TPU v7x, 256 devices: a 8x8x2 block of a 8x8x16 slice. The times are simulated.
256 devices in a mesh: groups: 2 (over z), tensor: 128 (over x, y, core).
Axes of the slice: x: 8, y: 8, z: 2, core: 2. Of those that a mesh axis runs over, the one named last changes fastest.
The devices are a block of a 8x8x16 slice.
Arguments:
- image_features: bfloat16 [256, 12800], P('groups', 'tensor'), parts along dimension 0, may hold values from -6 to 6
- image_counts: int32 [4], P('groups'), parts along dimension 0, may hold values from 1 to 64, 80 in all
- slot_position: int32 [256], P('groups'), parts along dimension 0, may hold values from 0 to 255, as said below
- text_ids: int32 [512], P('groups'), parts along dimension 0, may hold values from 0 to 49151
- norm_gain: float32 [12800], replicated, may hold values from 0.5 to 1.5
- norm_bias: float32 [12800], replicated, may hold values from -3 to 3
- proj_first: bfloat16 [6144, 12800], P('tensor'), may hold values from -0.0546875 to 0.0546875
- proj_second: bfloat16 [6144, 6144], P('tensor'), may hold values from -0.078125 to 0.078125
- embedding: bfloat16 [6144, 49152], P('tensor'), may hold values from -6 to 6
- rms_gain: float32 [6144], replicated, may hold values from 0.5 to 1.5
- gate_weight: bfloat16 [6144, 16384], P(None, 'tensor'), may hold values from -0.3125 to 0.3125
- up_weight: bfloat16 [6144, 16384], P(None, 'tensor'), may hold values from -0.3125 to 0.3125
- down_weight: bfloat16 [16384, 6144], P('tensor'), may hold values from -0.046875 to 0.046875
- output_grad: bfloat16 [512, 6144], P('groups', 'tensor'), parts along dimension 0, may hold values from -6 to 6
Outputs:
- input_grad: float32 [512, 6144], P('groups', 'tensor'), parts along dimension 0
- second_grad: float32 [12288, 6144], P(('groups', 'tensor')), parts along dimension 0
There are 2 independent parts, one for each index of `groups`. A program takes and returns all parts, laid end to end along the dimension named above; an argument that names none is the same for every part. Nothing has to cross between parts.
Inputs may be any that keep to these rules, and one draw needn't show every extreme that they name: `image_counts`: the counts sum to 80. `slot_position`: the 128 positions are distinct.
All inputs are finite; a program needn't handle non-finite values.
Results may differ from a plain program's by a relative error of at most 0.0079.
Values may be sent and summed in bfloat16 or wider, within the bound.
A program may use at most 128 MiB of HBM per device.

v0:
```python
import jax
import jax.numpy as jnp
from jax import lax
from jax.sharding import Mesh
from jax.sharding import PartitionSpec as P

LIVE = 80
TENSOR = ("tensor_0", "tensor_1", "tensor_2")
GROUPS_TENSOR = ("groups", "tensor_0", "tensor_1", "tensor_2")


def in_order(parts, dim):
    shape = list(parts.shape[1:])
    shape[dim] *= parts.shape[0]
    return jnp.moveaxis(parts, 0, dim).reshape(shape)


def all_blocks(x, axes, order):
    parts = x
    for k in order:
        parts = lax.all_gather(parts, axes[k])
    done = order[::-1]
    back = [done.index(k) for k in range(len(axes))]
    parts = parts.transpose(*back, *range(len(axes), parts.ndim))
    return parts.reshape(-1, *x.shape)


def whole_of(x, axes, order, dim):
    return in_order(all_blocks(x, axes, order), dim)


def own_block(parts, axes, order):
    inside = parts.shape[1:]
    parts = parts.reshape(*(lax.axis_size(a) for a in axes), *inside)
    parts = jnp.moveaxis(parts, order, range(len(axes))).reshape(-1, *inside)
    for k in order:
        parts = lax.psum_scatter(parts, axes[k], scatter_dimension=0, tiled=True)
    return parts[0]


def in_blocks(x, dim, size):
    before, after = (x.shape[:dim], x.shape[dim + 1 :])
    return jnp.moveaxis(x.reshape(*before, size, -1, *after), dim, 0)


def scatter_axes(x, axes, order, dim):
    size = lax.axis_size(axes)
    return own_block(in_blocks(x, dim, size), axes, order)


def one_axis_at_a_time(x, axes):
    for axis in axes:
        x = lax.psum(x, axis)
    return x


def layer_norm(rows_in, gain_in, bias_in):
    values = rows_in.astype(jnp.float32)
    centre = values - jnp.mean(values, axis=-1, keepdims=True)
    spread = jnp.mean(centre * centre, axis=-1, keepdims=True)
    return (centre * lax.rsqrt(spread + 1e-05) * gain_in + bias_in).astype(jnp.bfloat16)


def on_device(
    image_features,
    image_counts,
    slot_position,
    text_ids,
    norm_gain,
    norm_bias,
    proj_first,
    proj_second,
    embedding,
    rms_gain,
    gate_weight,
    up_weight,
    down_weight,
    output_grad,
):
    slot_total = image_features.shape[0]
    per_image = slot_total // image_counts.shape[0]
    seq_len = output_grad.shape[0]
    model_width = gate_weight.shape[0]
    col_count = output_grad.shape[1]
    slot_ids = jnp.arange(slot_total, dtype=jnp.int32)
    is_live = slot_ids % per_image < jnp.repeat(
        image_counts, per_image, total_repeat_length=slot_total
    )
    packed_order = jnp.argsort(jnp.where(is_live, 0, 1).astype(jnp.int32), stable=True)[:LIVE]
    gathered = whole_of(image_features[packed_order], TENSOR, (0, 1, 2), 1)
    positions = slot_position[packed_order]
    in_use = jnp.ones((LIVE,), dtype=bool)
    normed = layer_norm(gathered, norm_gain, norm_bias)
    hidden_pre = lax.dot_general(
        normed, proj_first, (((1,), (1,)), ((), ())), preferred_element_type=jnp.float32
    )
    act_cols = jax.nn.gelu(hidden_pre, approximate=False).astype(jnp.bfloat16)
    act_full = lax.all_gather(act_cols, TENSOR, axis=1, tiled=True)
    projected = lax.dot_general(
        act_full, proj_second, (((1,), (1,)), ((), ())), preferred_element_type=jnp.float32
    ).astype(jnp.bfloat16)
    target = jnp.where(in_use, positions, seq_len)
    text_rows = jnp.take(embedding, text_ids, axis=1).T
    tokens = text_rows.at[target].set(projected, mode="drop")
    full_tokens = lax.all_gather(tokens, TENSOR, axis=1, tiled=True)
    values = full_tokens.astype(jnp.float32)
    inverse = lax.rsqrt(jnp.mean(values * values, axis=-1, keepdims=True) + 1e-05)
    normed_tokens = (values * inverse * rms_gain).astype(jnp.bfloat16)
    gate_out = jnp.dot(normed_tokens, gate_weight, preferred_element_type=jnp.float32)
    up_out = jnp.dot(normed_tokens, up_weight, preferred_element_type=jnp.float32)
    hidden_grad = lax.dot_general(
        lax.all_gather(output_grad, TENSOR, axis=1, tiled=True),
        down_weight,
        (((1,), (1,)), ((), ())),
        preferred_element_type=jnp.float32,
    )
    sig_gate = jax.nn.sigmoid(gate_out)
    gate_grad = (hidden_grad * up_out * sig_gate * (1.0 + gate_out * (1.0 - sig_gate))).astype(
        jnp.bfloat16
    )
    up_grad = (hidden_grad * gate_out * sig_gate).astype(jnp.bfloat16)
    partial_value = lax.dot_general(
        gate_grad, gate_weight, (((1,), (1,)), ((), ())), preferred_element_type=jnp.float32
    )
    partial_value = partial_value + lax.dot_general(
        up_grad, up_weight, (((1,), (1,)), ((), ())), preferred_element_type=jnp.float32
    )
    norm_grad = scatter_axes(partial_value, TENSOR, (2, 0, 1), 1)
    offset = lax.axis_index(TENSOR) * col_count
    gain_cols = lax.dynamic_slice_in_dim(rms_gain, offset, col_count, 0)
    unit_cols = tokens.astype(jnp.float32) * inverse
    scaled = gain_cols * norm_grad
    row_sums = one_axis_at_a_time(jnp.sum(scaled * unit_cols, axis=-1), TENSOR)
    input_grad = output_grad.astype(jnp.float32) + inverse * (
        scaled - unit_cols * (row_sums / model_width)[:, None]
    )
    proj_grad = jnp.where(in_use[:, None], input_grad[positions], 0.0).astype(jnp.bfloat16)
    second_grad = lax.dot_general(
        proj_grad, act_full, (((0,), (0,)), ((), ())), preferred_element_type=jnp.float32
    )
    return (input_grad, second_grad)


def solution(mesh):
    torus = Mesh(
        mesh.devices.reshape(mesh.shape["groups"], 8, 8, 2),
        ("groups", "tensor_0", "tensor_1", "tensor_2"),
    )
    in_specs = (
        P("groups", TENSOR),
        P("groups"),
        P("groups"),
        P("groups"),
        P(),
        P(),
        P(TENSOR, None),
        P(TENSOR, None),
        P(TENSOR, None),
        P(),
        P(None, TENSOR),
        P(None, TENSOR),
        P(TENSOR, None),
        P("groups", TENSOR),
    )
    out_specs = (P("groups", TENSOR), P(GROUPS_TENSOR, None))
    return jax.shard_map(
        on_device, mesh=torus, in_specs=in_specs, out_specs=out_specs, check_vma=False
    )
```

profile of v0, /device:TPU:514, one launch (start us, length us, event | category | flops | bytes accessed | tf_op | source)
XLA Modules:
  0.0 527.0 jit_solution(11079233701716624059)
XLA Ops:
  7.3 1.4 fusion.34
  8.6 2.0 compare_select_fusion.3
  10.6 2.5 sort.17
  14.7 40.9 %all-gather = bf16[640,100]{1,0:T(8,128)(2,1)S(1)} all-gather(bf16[80,100]{1,0:T(8,128)(2,1)S(1)} %gather_fusion.2), channel_id=2, replica_groups=mesh['groups'=2,'tensor_0'=8,'tensor_1'=8,'tensor_2'=2] {'tensor_0'}, dimensions={0}, use_global_device_ids=true | all-gather | bytes 144000 | tf_op jit(solution)/shard_map/all_gather | solution.py:21
  55.6 28.6 %all-gather.1 = bf16[64,80,100]{2,1,0:T(8,128)(2,1)} all-gather(bf16[8,80,100]{2,1,0:T(8,128)(2,1)S(1)} %bitcast.49), channel_id=3, replica_groups=mesh['groups'=2,'tensor_0'=8,'tensor_1'=8,'tensor_2'=2] {'tensor_1'}, dimensions={0}, use_global_device_ids=true | all-gather | bytes 1152000 | tf_op jit(solution)/shard_map/all_gather | solution.py:21
  85.1 1.2 gather_fusion.1
  86.3 11.6 %copy.40 = bf16[48,49152]{0,1:T(8,128)(2,1)} copy(bf16[48,49152]{1,0:T(8,128)(2,1)} %param.24) | data formatting | bytes 9437184 | tf_op args[8]
  98.0 8.2 %gather_fusion = bf16[256,48]{1,0:T(8,128)(2,1)S(1)} fusion(bf16[48,49152]{0,1:T(8,128)(2,1)} %copy.40, s32[1024]{0:T(1024)S(1)} %pad_clamp_fusion.2), kind=kCustom, calls=%fused_computation | custom fusion | bytes 50176 | tf_op jit(solution)/shard_map/jit(_take)/gather | solution.py:103
  106.4 2.3 convert_element_type.79
  109.4 2.3 copy-done.3
  111.8 3.9 copy.43
  115.7 6.8 %reshape.107 = f32[80,12800]{1,0:T(8,128)} reshape(f32[80,128,100]{2,1,0:T(8,128)} %copy.43) | data formatting | bytes 8192000 | tf_op jit(solution)/shard_map/convert_element_type | solution.py:58
  122.5 2.5 convert_reduce_fusion
  125.1 3.5 fusion.4
  129.8 52.0 %all_gather.33 = bf16[80,6144]{0,1:T(8,128)(2,1)S(1)} all-gather(bf16[80,48]{0,1:T(8,128)(2,1)S(1)} %fusion.21), channel_id=1, replica_groups=mesh['groups'=2,'tensor_0'=8,'tensor_1'=8,'tensor_2'=2] {'tensor_0','ten..., dimensions={1}, use_global_device_ids=true | all-gather | bytes 990720 | tf_op jit(solution)/shard_map/all_gather | solution.py:98
  184.2 4.8 all-gather.9.cloned.1.call-done
  189.0 3.4 fusion.35
  192.4 78.0 %all-gather.7.cloned.1.call-done = bf16[256,6144]{0,1:T(8,128)(2,1)} async-done(((bf16[256,48]{0,1:T(8,128)(2,1)}), bf16[256,6144]{0,1:T(8,128)(2,1)}) %all-gather.7.cloned.1.call-update) | async-done | bytes 3145744 | tf_op jit(solution)/shard_map/all_gather | solution.py:105
  270.4 2.9 fusion
  273.3 3.4 fusion.10
  276.8 8.1 %fusion.9 = f32[256,6144]{1,0:T(8,128)} fusion(bf16[6144,128]{1,0:T(8,128)(2,1)} %param.26, f32[256,128]{1,0:T(8,128)S(1)} %fusion.35, bf16[6144,128]{1,0:T(8,128)(2,1)S(1)} %copy-done, bf16[256,6144]{0,1:T(8,128)(2,1)} %all-gather.7.cloned.1.call-done, f32[6144]{0:T(1024)S(1)} %copy-done.8, f32[256]{0:T(256)S(1)} %add_rsqrt_fusion, f32[256,128]{1,0:T(8,128)S(1)} %fusion.10), kind=kOutput, calls=%fused_computation.21 | convolution fusion | flops 811925504 | bytes 12870656 | tf_op jit(solution)/shard_map/dot_general | solution.py:122
  284.8 6.4 %convolution_add_fusion = f32[256,6144]{1,0:T(8,128)} fusion(f32[256,6144]{1,0:T(8,128)} %fusion.9, bf16[6144,128]{1,0:T(8,128)(2,1)S(1)} %copy-done, f32[256,128]{1,0:T(8,128)S(1)} %fusion.35, f32[256,128]{1,0:T(8,128)S(1)} %fusion.10), kind=kOutput, calls=%fused_computation.5 | convolution fusion | flops 404422656 | bytes 14417920 | tf_op jit(solution)/shard_map/dot_general | solution.py:125
  291.2 6.6 %copy.46 = f32[256,6144]{0,1:T(8,128)} copy(f32[256,6144]{1,0:T(8,128)} %convolution_add_fusion) | data formatting | bytes 12582912 | tf_op jit(solution)/shard_map/add | solution.py:125
  297.8 11.5 %copy.47 = f32[8,8,2,256,48]{4,3,1,0,2:T(8,128)} copy(f32[8,8,2,256,48]{3,4,2,1,0:T(8,128)} %bitcast.46) | data formatting | bytes 12582912 | tf_op jit(solution)/shard_map/reshape | solution.py:34
  309.5 30.2 %reduce-scatter.4.cloned.1.call-done = f32[64,256,48]{2,1,0:T(8,128)} async-done(((f32[128,256,48]{2,1,0:T(8,128)}), f32[64,256,48]{2,1,0:T(8,128)}) %reduce-scatter.4.cloned.1.call-update) | async-done | bytes 3145744 | tf_op jit(solution)/shard_map/reduce_scatter | solution.py:37
  339.8 98.2 %reduce-scatter.6.cloned.1.call-done = f32[8,256,48]{2,1,0:T(8,128)} async-done(((f32[64,256,48]{2,1,0:T(8,128)}), f32[8,256,48]{2,1,0:T(8,128)}) %reduce-scatter.6.cloned.1.call-update) | async-done | bytes 393232 | tf_op jit(solution)/shard_map/reduce_scatter | solution.py:37
  438.3 43.0 %reduce-scatter.8.cloned.1.call-done = f32[1,256,48]{2,1,0:T(8,128)} async-done(((f32[8,256,48]{2,1,0:T(8,128)}), f32[1,256,48]{2,1,0:T(8,128)}) %reduce-scatter.8.cloned.1.call-update) | async-done | bytes 49168 | tf_op jit(solution)/shard_map/reduce_scatter | solution.py:37
  481.3 1.1 multiply_reduce_fusion
  482.4 15.7 %psum.21 = f32[256]{0:T(256)S(1)} all-reduce(f32[256]{0:T(256)S(1)} %multiply_reduce_fusion), channel_id=1, replica_groups=mesh['groups'=2,'tensor_0'=8,'tensor_1'=8,'tensor_2'=2] {'tensor_0'}, use_global_device_ids=true, to_apply=%region_9.10 | all-reduce | flops 256 | bytes 2048 | tf_op jit(solution)/shard_map/psum | solution.py:53
  498.1 15.5 %psum.22 = f32[256]{0:T(256)S(1)} all-reduce(f32[256]{0:T(256)S(1)} %psum.21), channel_id=1, replica_groups=mesh['groups'=2,'tensor_0'=8,'tensor_1'=8,'tensor_2'=2] {'tensor_1'}, use_global_device_ids=true, to_apply=%region_10.11 | all-reduce | flops 256 | bytes 2048 | tf_op jit(solution)/shard_map/psum | solution.py:53
  513.6 2.5 psum.23
  518.5 1.7 fusion.36
  (64 shorter events, 9.9 us)
Async XLA Ops:
  7.2 269.6 %copy-start = (bf16[6144,128]{1,0:T(8,128)(2,1)S(1)}, bf16[6144,128]{1,0:T(8,128)(2,1)}, u32[]{:S(2)}) copy-start(bf16[6144,128]{1,0:T(8,128)(2,1)} %param.27) | copy-start | bytes 4718596
  7.2 77.9 %copy-start.2 = (s32[128]{0:T(128)S(1)}, s32[128]{0:T(128)}, u32[]{:S(2)}) copy-start(s32[128]{0:T(128)} %param.18) | copy-start | bytes 1540
  7.2 99.2 %all-gather.11.cloned.1.call-start = ((), (), s32[]{:S(2)}) async-start(), calls=%async_computation.8 | async-start | bytes 3932160 | tf_op jit(solution)/shard_map/all_gather | solution.py:21
  84.2 104.8 %all-gather.9.cloned.1.call-start = ((), (), s32[]{:S(2)}) async-start(), calls=%async_computation.4 | async-start | bytes 3170304 | tf_op jit(solution)/shard_map/all_gather | solution.py:112
  85.0 185.4 %all-gather.7.cloned.1.call-start = ((), (), s32[]{:S(2)}) async-start(), calls=%async_computation.3 | async-start | bytes 3170304 | tf_op jit(solution)/shard_map/all_gather | solution.py:105
  86.3 11.6 %copy-start.9 = (s32[256]{0:T(256)S(1)}, s32[256]{0:T(256)}, u32[]{:S(2)}) copy-start(s32[256]{0:T(256)} %param.19) | copy-start | bytes 3076
  109.4 2.3 copy-start.3
  122.5 6.1 %copy-start.10 = (bf16[48,12800]{1,0:T(8,128)(2,1)S(1)}, bf16[48,12800]{1,0:T(8,128)(2,1)}, u32[]{:S(2)}) copy-start(bf16[48,12800]{1,0:T(8,128)(2,1)} %param.22) | copy-start | bytes 3686404
  125.0 3.7 copy-start.5
  125.0 3.7 copy-start.11
  125.0 3.7 copy-start.12
  128.7 53.1 %copy-start.6 = (bf16[48,6144]{1,0:T(8,128)(2,1)S(1)}, bf16[48,6144]{1,0:T(8,128)(2,1)}, u32[]{:S(2)}) copy-start(bf16[48,6144]{1,0:T(8,128)(2,1)} %param.23) | copy-start | bytes 1769476
  183.9 89.3 %copy-start.8 = (f32[6144]{0:T(1024)S(1)}, f32[6144]{0:T(1024)}, u32[]{:S(2)}) copy-start(f32[6144]{0:T(1024)} %param.25) | copy-start | bytes 73732
  183.9 155.8 %reduce-scatter.4.cloned.1.call-start = ((), (), s32[]{:S(2)}) async-start(), calls=%async_computation.5 | async-start | bytes 25165824 | tf_op jit(solution)/shard_map/reduce_scatter | solution.py:37
  270.4 2.9 copy-start.4
  309.4 128.6 %reduce-scatter.6.cloned.1.call-start = ((), (), s32[]{:S(2)}) async-start(), calls=%async_computation.6 | async-start | bytes 9437184 | tf_op jit(solution)/shard_map/reduce_scatter | solution.py:37
  339.7 98.4 %copy-start.7 = (bf16[256,48]{0,1:T(8,128)(2,1)S(1)}, bf16[256,48]{0,1:T(8,128)(2,1)}, u32[]{:S(2)}) copy-start(bf16[256,48]{0,1:T(8,128)(2,1)} %param.29) | copy-start | bytes 73732
  339.8 180.4 %copy-start.1 = (bf16[6144,128]{1,0:T(8,128)(2,1)S(1)}, bf16[6144,128]{1,0:T(8,128)(2,1)}, u32[]{:S(2)}) copy-start(bf16[6144,128]{1,0:T(8,128)(2,1)} %param.27) | copy-start | bytes 4718596
  339.8 141.5 %reduce-scatter.8.cloned.1.call-start = ((), (), s32[]{:S(2)}) async-start(), calls=%async_computation.7 | async-start | bytes 1179648 | tf_op jit(solution)/shard_map/reduce_scatter | solution.py:37
Sparse Core Ops, SparseCore 0:
  84.3 20.4 all-gather.10
  107.4 81.5 all-gather.8
  192.2 78.1 all-gather.6
  309.6 30.0 reduce-scatter.3
  342.1 95.8 reduce-scatter.5
  440.4 40.8 reduce-scatter.7
where the time goes:
time: 531 us; the launch traced here: 527 us
  waiting for transfers between devices  255 us (48%)
  blocking collectives  155 us (29%)
  local copies, waits for them, and re-layouts  59.2 us (11%)
  matrix products  24.4 us (5%)
  other arithmetic  18 us (3%)
  between operations  14.4 us (3%)
    reduce_scatter x3, waiting for transfers between devices, own_block(): parts = lax.psum_scatter(parts, axes[k], scatter_dimension=0, tiled=True)  171 us
    all_gather x1, waiting for transfers between devices, on_device(): full_tokens = lax.all_gather(tokens, TENSOR, axis=1, tiled=True)  78 us
    all_gather x2, blocking collectives, all_blocks(): parts = lax.all_gather(parts, axes[k])  69.5 us
    all_gather x1, blocking collectives, on_device(): act_full = lax.all_gather(act_cols, TENSOR, axis=1, tiled=True)  52 us
    psum x3, blocking collectives, one_axis_at_a_time(): x = lax.psum(x, axis)  33.7 us
    unnamed x30, local copies, waits for them, and re-layouts  15.8 us
    reshape x1, local copies, waits for them, and re-layouts, own_block(): parts = parts.reshape(*(lax.axis_size(a) for a in axes), *inside)  11.5 us
    convert_element_type x3, local copies, waits for them, and re-layouts, layer_norm(): values = rows_in.astype(jnp.float32)  11.5 us
  transfers between devices with their start and end apart: 6, of which 5 were waited for; matrix products, arithmetic and copies ran while one was open for 9% of the time, Pallas kernels for 0%

commit v1 on v0

v1 whole, which is shorter than its diff:
```python
import jax
import jax.numpy as jnp
from jax import lax
from jax.experimental import pallas as pl
from jax.experimental.pallas import tpu as pltpu
from jax.sharding import Mesh
from jax.sharding import PartitionSpec as P

LIVE = 80
TENSOR = ("tensor_0", "tensor_1", "tensor_2")
GROUPS_TENSOR = ("groups", "tensor_0", "tensor_1", "tensor_2")
MESH = pl.DeviceIdType.MESH
F32 = jnp.float32
BF16 = jnp.bfloat16
NT = (((1,), (1,)), ((), ()))
NN = (((1,), (0,)), ((), ()))
LANES = 128


def dot(a, b, dims=NN):
    return lax.dot_general(a, b, dims, preferred_element_type=F32)


def erf(x):
    x = jnp.clip(x, -3.832506856900711, 3.832506856900711)
    s = x * x
    top = jnp.full_like(x, 0.00022905065861350646)
    for k in (
        0.0034082910107109506,
        0.050955695062380861,
        0.18520832239976145,
        1.128379143519084,
    ):
        top = top * s + k
    low = jnp.full_like(x, -1.1791602954361697e-7)
    for k in (
        0.000023547966471313185,
        0.0010179625278914885,
        0.014070470171167667,
        0.11098505178285362,
        0.49746925110067538,
        1.0,
    ):
        low = low * s + k
    return x * top / low


class Torus:
    def __init__(self):
        self.c = lax.axis_index("tensor_2")
        self.x = lax.axis_index("tensor_0")
        self.y = lax.axis_index("tensor_1")
        self.n = lax.axis_size("tensor_0")
        self.p = self.pick(self.x, self.y)
        self.q = self.pick(self.y, self.x)
        self.me = self.block(self.p, self.q)
        self.partner = {"tensor_0": self.x, "tensor_1": self.y, "tensor_2": 1 - self.c}

    def pick(self, a, b):
        return (1 - self.c) * a + self.c * b

    def dev(self, p, q):
        return {"tensor_0": self.pick(p, q), "tensor_1": self.pick(q, p), "tensor_2": self.c}

    def chip(self, p, q):
        return self.pick(p, q) * self.n + self.pick(q, p)

    def block(self, p, q):
        return self.chip(p, q) * 2 + self.c

    def turn(self, a, d):
        return lax.rem(a + d + self.n, self.n)


class Gather:
    def __init__(self, t, buf, near, plus, minus, mate, sent):
        self.t, self.buf = t, buf
        self.near, self.plus, self.minus, self.mate, self.sent = near, plus, minus, mate, sent

    def copy(self, j, dev, sem):
        return pltpu.make_async_remote_copy(
            self.buf.at[j], self.buf.at[j], self.sent, sem, device_id=dev, device_id_type=MESH
        )

    def to_mate(self, j):
        self.copy(j, self.t.partner, self.mate.at[0]).start()

    def got(self, j, sem):
        self.copy(j, self.t.partner, sem).wait_recv()

    def start(self):
        t = self.t

        @pl.loop(1, t.n)
        def _(d):
            self.copy(t.me, t.dev(t.turn(t.p, d), t.q), self.near.at[d]).start()

        self.to_mate(t.me)

    def ring(self, j, d, hop, up, down):
        t = self.t
        if up:
            self.copy(j, t.dev(t.p, t.turn(t.q, 1)), self.plus.at[hop, d]).start()
        if down:
            self.copy(j, t.dev(t.p, t.turn(t.q, -1)), self.minus.at[hop, d]).start()

    def hop0(self):
        t = self.t
        self.ring(t.me, 0, 0, True, True)

        @pl.loop(1, t.n)
        def _(d):
            j = t.block(t.turn(t.p, -d), t.q)
            self.got(j, self.near.at[d])
            self.ring(j, d, 0, True, True)
            self.to_mate(j)

    def hop(self, h):
        t = self.t
        half = t.n // 2

        def up(d, on):
            j = t.block(t.turn(t.p, -d), t.turn(t.q, -h))
            self.got(j, self.plus.at[h - 1, d])
            self.ring(j, d, h, on, False)
            self.to_mate(j)

        def down(d, on):
            j = t.block(t.turn(t.p, -d), t.turn(t.q, h))
            self.got(j, self.minus.at[h - 1, d])
            self.ring(j, d, h, False, on)
            self.to_mate(j)

        if h < half - 1:

            @pl.loop(0, t.n)
            def _(d):
                up(d, True)
                down(d, True)

        elif h == half - 1:

            @pl.loop(0, half)
            def _(d):
                up(d, True)
                down(d + half, True)
                down(d, False)
                up(d + half, False)

        else:

            @pl.loop(0, half)
            def _(d):
                up(d, False)
                down(d + half, False)

    def finish(self):
        half = self.buf.at[pl.ds(0, self.buf.shape[0] // 2)]
        pltpu.make_async_remote_copy(
            half, half, self.sent, self.mate.at[0], device_id=self.t.partner, device_id_type=MESH
        ).wait_recv()

    def drain(self):
        most = self.buf.at[pl.ds(0, self.buf.shape[0] - 1)]
        pltpu.make_async_remote_copy(
            most, most, self.sent, self.mate.at[0], device_id=self.t.partner, device_id_type=MESH
        ).wait_send()


class Scatter:
    def __init__(self, t, part, give, take, out_up, out_dn, in_up, in_dn, fin_out, fin_in, sems):
        self.t, self.part, self.give, self.take = t, part, give, take
        self.out_up, self.out_dn, self.in_up, self.in_dn = out_up, out_dn, in_up, in_dn
        self.fin_out, self.fin_in = fin_out, fin_in
        self.sent, self.mate, self.s_up, self.s_dn, self.s_fin = sems

    def mate_copy(self):
        return pltpu.make_async_remote_copy(
            self.give,
            self.take,
            self.sent.at[0],
            self.mate.at[0],
            device_id=self.t.partner,
            device_id_type=MESH,
        )

    def start(self):
        t = self.t

        @pl.loop(0, self.give.shape[0])
        def _(i):
            self.give[i] = self.part[2 * i + 1 - t.c].astype(BF16)

        self.mate_copy().start()

    def mated(self):
        self.mate_copy().wait_recv()

    def base(self, p, q):
        t = self.t
        i = t.chip(p, q)
        return self.part[2 * i + t.c] + self.take[i].astype(F32)

    def up_copy(self, s, d):
        t = self.t
        return pltpu.make_async_remote_copy(
            self.out_up.at[s, d],
            self.in_up.at[s, d],
            self.sent.at[0],
            self.s_up.at[s, d],
            device_id=t.dev(t.p, t.turn(t.q, 1)),
            device_id_type=MESH,
        )

    def dn_copy(self, s, d):
        t = self.t
        return pltpu.make_async_remote_copy(
            self.out_dn.at[s, d],
            self.in_dn.at[s, d],
            self.sent.at[0],
            self.s_dn.at[s, d],
            device_id=t.dev(t.p, t.turn(t.q, -1)),
            device_id_type=MESH,
        )

    def step(self, s):
        t = self.t
        half = t.n // 2
        far = half - s

        def up(d, had):
            value = self.base(t.turn(t.p, -d), t.turn(t.q, far))
            if had:
                self.up_copy(s - 1, d).wait_recv()
                value = value + self.in_up[s - 1, d].astype(F32)
            self.out_up[s, d] = value.astype(BF16)
            self.up_copy(s, d).start()

        def dn(d, had):
            value = self.base(t.turn(t.p, -d), t.turn(t.q, -far))
            if had:
                self.dn_copy(s - 1, d).wait_recv()
                value = value + self.in_dn[s - 1, d].astype(F32)
            self.out_dn[s, d] = value.astype(BF16)
            self.dn_copy(s, d).start()

        if s == 0:

            @pl.loop(0, half)
            def _(d):
                up(d, False)
                dn(d + half, False)

        elif s == 1:

            @pl.loop(0, half)
            def _(d):
                up(d, True)
                dn(d + half, True)
                up(d + half, False)
                dn(d, False)

        else:

            @pl.loop(0, t.n)
            def _(d):
                up(d, True)
                dn(d, True)

    def fin_copy(self, d):
        t = self.t
        return pltpu.make_async_remote_copy(
            self.fin_out.at[d],
            self.fin_in.at[d],
            self.sent.at[0],
            self.s_fin.at[d],
            device_id=t.dev(t.turn(t.p, -d), t.q),
            device_id_type=MESH,
        )

    def whole(self, d):
        t = self.t
        last = t.n // 2 - 1
        value = self.base(t.turn(t.p, -d), t.q)
        self.up_copy(last, d).wait_recv()
        self.dn_copy(last, d).wait_recv()
        return value + self.in_up[last, d].astype(F32) + self.in_dn[last, d].astype(F32)

    def last(self):
        t = self.t

        @pl.loop(1, t.n)
        def _(d):
            self.fin_out[d] = self.whole(d).astype(BF16)
            self.fin_copy(d).start()

        return self.whole(0)

    def collect(self, value):
        for d in range(1, self.t.n):
            self.fin_copy(d).wait_recv()
            value = value + self.fin_in[d].astype(F32)
        return value

    def drain(self, like):
        most = like.at[pl.ds(0, like.shape[0] - 1)]
        pltpu.make_async_remote_copy(
            most, most, self.sent.at[0], self.mate.at[0], device_id=self.t.partner, device_id_type=MESH
        ).wait_send()


def kernel_body(
    feats_ref,
    counts_ref,
    pos_ref,
    ids_ref,
    ngain_ref,
    nbias_ref,
    first_hbm,
    second_hbm,
    emb_hbm,
    rgain_ref,
    gate_hbm,
    up_hbm,
    down_hbm,
    og_ref,
    igrad_ref,
    sgrad_ref,
    first_v,
    second_v,
    emb_v,
    wcat,
    down_v,
    wt,
    wpad,
    gpad,
    bpad,
    normed,
    feats_all,
    act_all,
    og_all,
    ta_all,
    tb_all,
    text_own,
    part,
    give,
    take,
    out_up,
    out_dn,
    in_up,
    in_dn,
    fin_out,
    fin_in,
    rd_own,
    rd_mate,
    rd_p,
    rd_pin,
    rd_q,
    rd_qin,
    load_sem,
    near_sem,
    plus_sem,
    minus_sem,
    mate_sem,
    sent_sem,
    rs_sent,
    rs_mate,
    rs_up,
    rs_dn,
    rs_fin,
    rd_sent,
    rd_recv_p,
    rd_recv_q,
    rd_recv_m,
):
    t = Torus()
    n = t.n
    blocks = 2 * n * n
    cols, seq = og_ref.shape
    width, slots = feats_ref.shape
    model = blocks * cols
    pix = blocks * width
    text_b = LANES - LIVE

    loads = [
        pltpu.make_async_copy(first_hbm, first_v, load_sem.at[0]),
        pltpu.make_async_copy(gate_hbm, wcat.at[:, pl.ds(0, LANES)], load_sem.at[1]),
        pltpu.make_async_copy(up_hbm, wcat.at[:, pl.ds(LANES, LANES)], load_sem.at[2]),
        pltpu.make_async_copy(second_hbm, second_v, load_sem.at[3]),
        pltpu.make_async_copy(down_hbm, down_v, load_sem.at[4]),
    ]
    loads[0].start()

    @pl.loop(0, emb_v.shape[0])
    def _(k):
        span = pl.ds(pl.multiple_of(k * LANES, LANES), LANES)
        pltpu.make_async_copy(emb_hbm.at[:, span], emb_v.at[k], load_sem.at[5]).start()

    for load in loads[1:]:
        load.start()

    barrier = pltpu.get_barrier_semaphore()

    @pl.loop(1, n)
    def _(d):
        pl.semaphore_signal(
            barrier, inc=1, device_id=t.dev(t.turn(t.p, d), t.q), device_id_type=MESH
        )
        pl.semaphore_signal(
            barrier, inc=1, device_id=t.dev(t.p, t.turn(t.q, d)), device_id_type=MESH
        )

    pl.semaphore_signal(barrier, inc=1, device_id=t.partner, device_id_type=MESH)

    slot = lax.broadcasted_iota(jnp.int32, (LIVE, slots), 1)
    row = lax.broadcasted_iota(jnp.int32, (LIVE, slots), 0)
    images = counts_ref.shape[0]
    per = slots // images
    at = slot % per
    live = jnp.zeros((LIVE, slots), jnp.int32)
    rank = at
    before = 0
    for k in range(images):
        count = counts_ref[k]
        here = (slot // per) == k
        live = jnp.where(here & (at < count), 1, live)
        rank = jnp.where(here, at + before, rank)
        before = before + count
    choose = jnp.where((live == 1) & (rank == row), 1.0, 0.0).astype(BF16)
    feats_own = dot(choose, feats_ref[...], NT)
    feats_all[t.me] = jnp.zeros((LIVE, LANES), BF16)
    feats_all[t.me, :, 0:width] = feats_own.astype(BF16)

    gathers = []
    for k, buf in enumerate((feats_all, og_all, ta_all, act_all, tb_all)):
        gathers.append(
            Gather(
                t,
                buf,
                near_sem.at[k],
                plus_sem.at[k],
                minus_sem.at[k],
                mate_sem.at[k],
                sent_sem.at[k],
            )
        )
    g_feats, g_og, g_ta, g_act, g_tb = gathers

    pl.semaphore_wait(barrier, 2 * (n - 1) + 1)
    g_feats.start()

    pos = pos_ref[...]
    where_row = lax.broadcasted_iota(jnp.int32, (seq, slots), 0)
    hit = jnp.where((where_row == pos) & (live[0:1] == 1), 1.0, 0.0)
    is_img = jnp.sum(hit, axis=1, keepdims=True)
    img_rank = jnp.sum(hit * rank[0:1].astype(F32), axis=1, keepdims=True)
    low = jnp.where(
        lax.broadcasted_iota(jnp.int32, (seq, seq), 1)
        < lax.broadcasted_iota(jnp.int32, (seq, seq), 0),
        1.0,
        0.0,
    ).astype(BF16)
    not_img = jnp.broadcast_to(1.0 - is_img, (seq, LANES)).astype(BF16)
    text_rank = dot(low, not_img)[:, 0:1]
    text_col = jnp.where(text_rank < LANES, text_rank, text_rank + LIVE)
    col_of = jnp.where(is_img > 0.5, LANES + img_rank, text_col)
    perm = jnp.where(
        lax.broadcasted_iota(jnp.int32, (seq, seq), 1).astype(F32) == col_of, 1.0, 0.0
    ).astype(BF16)
    og_packed = dot(og_ref[...], perm).astype(BF16)
    og_all[t.me] = og_packed
    g_og.start()

    loads[0].wait()
    wpad[...] = jnp.zeros(wpad.shape, BF16)
    gpad[...] = jnp.zeros(gpad.shape, F32)
    bpad[...] = jnp.zeros(bpad.shape, F32)
    for j in range(blocks):
        wpad[:, LANES * j : LANES * j + width] = first_v[:, width * j : width * (j + 1)]
        gpad[j : j + 1, 0:width] = ngain_ref[:, width * j : width * (j + 1)]
        bpad[j : j + 1, 0:width] = nbias_ref[:, width * j : width * (j + 1)]

    g_feats.hop0()

    pltpu.make_async_copy(emb_v, emb_v, load_sem.at[5]).wait()
    lane = lax.broadcasted_iota(jnp.int32, (cols, LANES), 1)

    def embed(tile):
        def one(k, acc):
            word = ids_ref[tile * LANES + k]
            inside = lax.rem(word, LANES)
            found = emb_v[lax.div(word, LANES)].astype(F32)
            column = jnp.sum(jnp.where(lane == inside, found, 0.0), axis=1, keepdims=True)
            return jnp.where(lane == k, column, acc)

        text_own[:, pl.ds(tile * LANES, LANES)] = lax.fori_loop(
            0, LANES, one, jnp.zeros((cols, LANES), F32), unroll=8
        ).astype(BF16)

    embed(0)
    g_feats.hop(1)
    embed(1)
    text_packed = dot(text_own[...], perm)
    text_a = text_packed[:, 0:LANES]
    text_b_tile = text_packed[:, LANES : 2 * LANES]
    ta_all[t.me] = text_a.astype(BF16)
    g_feats.hop(2)
    g_ta.start()

    loads[1].wait()
    loads[2].wait()
    big_eye = jnp.where(
        lax.broadcasted_iota(jnp.int32, (seq, seq), 1)
        == lax.broadcasted_iota(jnp.int32, (seq, seq), 0),
        1.0,
        0.0,
    ).astype(BF16)

    def turn_weights(a, b):
        @pl.loop(a, b)
        def _(k):
            at_row = pl.multiple_of(k * seq, seq)
            flipped = dot(big_eye, wcat[pl.ds(at_row, seq), :], NT)
            wt[:, pl.ds(at_row, seq)] = (flipped * rgain_ref[:, pl.ds(at_row, seq)]).astype(BF16)

    pieces = model // seq
    turn_weights(0, pieces // 2)
    g_feats.hop(3)
    g_og.hop0()
    turn_weights(pieces // 2, pieces)
    g_feats.hop(4)
    g_feats.finish()

    def add_up(k, acc):
        return acc + feats_all[k].astype(F32)

    zero = jnp.zeros((LIVE, LANES), F32)
    total = lax.fori_loop(0, blocks, add_up, zero, unroll=8)
    mean = jnp.sum(total, axis=1, keepdims=True) / pix

    def add_squares(k, acc):
        centre = feats_all[k].astype(F32) - mean
        return acc + centre * centre

    squares = lax.fori_loop(0, blocks, add_squares, zero, unroll=8)
    inside = lax.broadcasted_iota(jnp.int32, (LIVE, LANES), 1) < width
    spread = jnp.sum(jnp.where(inside, squares, 0.0), axis=1, keepdims=True) / pix
    scale = lax.rsqrt(spread + 1e-05)

    @pl.loop(0, blocks)
    def _(k):
        centre = feats_all[k].astype(F32) - mean
        value = centre * scale * gpad[pl.ds(k, 1), :] + bpad[pl.ds(k, 1), :]
        normed[:, pl.ds(pl.multiple_of(k * LANES, LANES), LANES)] = value.astype(BF16)

    depth = 8 * LANES

    def first_step(k, acc):
        span = pl.ds(pl.multiple_of(k * depth, depth), depth)
        return acc + dot(wpad[:, span], normed[:, span], NT)

    hidden = lax.fori_loop(
        0, blocks * LANES // depth, first_step, jnp.zeros((cols, LIVE), F32), unroll=2
    )
    hidden = 0.5 * hidden * (1.0 + erf(hidden * 0.7071067811865476))
    act_all[t.me] = jnp.zeros((cols, LANES), BF16)
    act_all[t.me, :, 0:LIVE] = hidden.astype(BF16)
    g_act.start()

    g_og.hop(1)
    g_act.hop0()
    g_og.hop(2)
    g_act.hop(1)
    g_ta.hop0()
    g_act.hop(2)
    g_og.hop(3)
    g_act.hop(3)
    g_act.hop(4)
    g_act.finish()

    loads[3].wait()
    group = blocks // 8
    span_rows = group * cols

    def rows_of(buf, k):
        return buf[pl.ds(k * group, group)].reshape(span_rows, buf.shape[2])

    def second_step(k, acc):
        span = pl.ds(pl.multiple_of(k * span_rows, span_rows), span_rows)
        return acc + dot(second_v[:, span], rows_of(act_all, k))

    projected = lax.fori_loop(0, 8, second_step, jnp.zeros((cols, LANES), F32))
    tb_all[t.me] = jnp.where(lane < LIVE, projected, text_b_tile).astype(BF16)
    g_tb.start()

    g_og.hop(4)
    g_ta.hop(1)
    g_tb.hop0()
    g_ta.hop(2)
    g_tb.hop(1)
    g_ta.hop(3)
    g_tb.hop(2)
    g_ta.hop(4)
    g_tb.hop(3)
    g_og.finish()
    loads[4].wait()

    def down_step(k, acc):
        span = pl.ds(pl.multiple_of(k * span_rows, span_rows), span_rows)
        return acc + dot(down_v[:, span], rows_of(og_all, k))

    hidden_grad = lax.fori_loop(0, 8, down_step, jnp.zeros((LANES, seq), F32))
    g_ta.finish()

    scatters = []
    for k in range(2):
        scatters.append(
            Scatter(
                t,
                part.at[k],
                give.at[k],
                take.at[k],
                out_up.at[k],
                out_dn.at[k],
                in_up.at[k],
                in_dn.at[k],
                fin_out.at[k],
                fin_in.at[k],
                (rs_sent.at[k], rs_mate.at[k], rs_up.at[k], rs_dn.at[k], rs_fin.at[k]),
            )
        )
    s_a, s_b = scatters

    def gated(buf, hid, k_part):
        def step(k, carry):
            acc, sq = carry
            rows = rows_of(buf, k)
            span = pl.ds(pl.multiple_of(k * span_rows, span_rows), span_rows)
            wide = rows.astype(F32)
            sq = sq + jnp.sum(wide * wide, axis=0, keepdims=True)
            return acc + dot(wt[:, span], rows), sq

        acc, sq = lax.fori_loop(
            0, 8, step, (jnp.zeros((2 * LANES, LANES), F32), jnp.zeros((1, LANES), F32))
        )
        inv = lax.rsqrt(sq / model + 1e-05)
        acc = acc * inv
        gate, up = acc[0:LANES], acc[LANES : 2 * LANES]
        sig = 1.0 / (1.0 + jnp.exp(-gate))
        gate_grad = (hid * up * sig * (1.0 + gate * (1.0 - sig))).astype(BF16)
        up_grad = (hid * gate * sig).astype(BF16)
        dots = jnp.sum(
            gate_grad.astype(F32) * gate + up_grad.astype(F32) * up, axis=0, keepdims=True
        )
        both = jnp.concatenate([gate_grad, up_grad], axis=0)

        @pl.loop(0, 8)
        def _(k):
            at_row = pl.multiple_of(k * span_rows, span_rows)
            value = dot(wcat[pl.ds(at_row, span_rows), :], both)
            part[k_part, pl.ds(k * group, group)] = value.reshape(group, cols, LANES)

        return inv, dots

    inv_a, dots_a = gated(ta_all, hidden_grad[:, 0:LANES], 0)
    s_a.start()
    g_tb.hop(4)
    s_a.mated()
    s_a.step(0)
    g_tb.finish()
    s_a.step(1)
    inv_b, dots_b = gated(tb_all, hidden_grad[:, LANES : 2 * LANES], 1)
    s_b.start()

    rd_own[...] = jnp.zeros(rd_own.shape, F32)
    rd_own[0:1] = dots_a
    rd_own[1:2] = dots_b

    def rd_copy(src, dst, sem_at, recv, dev):
        return pltpu.make_async_remote_copy(
            src, dst, rd_sent.at[sem_at], recv, device_id=dev, device_id_type=MESH
        )

    def rd_m():
        return rd_copy(rd_own, rd_mate, 0, rd_recv_m.at[0], t.partner)

    def rd_along_p(d):
        return rd_copy(rd_p, rd_pin.at[d], 1, rd_recv_p.at[d], t.dev(t.turn(t.p, d), t.q))

    def rd_along_q(d):
        return rd_copy(rd_q, rd_qin.at[d], 2, rd_recv_q.at[d], t.dev(t.p, t.turn(t.q, d)))

    rd_m().start()
    s_b.mated()
    s_b.step(0)
    rd_m().wait_recv()
    rd_p[...] = rd_own[...] + rd_mate[...]

    @pl.loop(1, n)
    def _(d):
        rd_along_p(d).start()

    s_a.step(2)
    s_b.step(1)
    rd_sum = rd_p[...]
    for d in range(1, n):
        rd_along_p(d).wait_recv()
        rd_sum = rd_sum + rd_pin[d]
    rd_q[...] = rd_sum

    @pl.loop(1, n)
    def _(d):
        rd_along_q(d).start()

    s_a.step(3)
    s_b.step(2)
    sum_a = s_a.last()
    s_b.step(3)
    rd_all = rd_q[...]
    for d in range(1, n):
        rd_along_q(d).wait_recv()
        rd_all = rd_all + rd_qin[d]
    own = lax.broadcasted_iota(jnp.int32, (cols, model), 1) == (
        lax.broadcasted_iota(jnp.int32, (cols, model), 0) + t.me * cols
    )
    gain_own = jnp.sum(jnp.where(own, rgain_ref[...], 0.0), axis=1, keepdims=True)
    sum_b = s_b.last()
    grad_a = s_a.collect(sum_a)
    grad_b = s_b.collect(sum_b)

    def update(grad, tokens, inv, dots):
        unit = tokens.astype(F32) * inv
        return inv * (gain_own * grad - unit * (dots / model))

    upd_a = update(grad_a, ta_all[t.me], inv_a, rd_all[0:1])
    upd_b = update(grad_b, tb_all[t.me], inv_b, rd_all[1:2])
    grad_img = og_all[t.me, :, LANES : 2 * LANES].astype(F32) + upd_b
    proj_grad = jnp.where(lane < LIVE, grad_img, 0.0).astype(BF16)

    @pl.loop(0, 8)
    def _(k):
        span = pl.ds(pl.multiple_of(k * span_rows, span_rows), span_rows)
        sgrad_ref[:, span] = dot(proj_grad, rows_of(act_all, k), NT)

    upd = jnp.concatenate([upd_a, upd_b], axis=1)
    high = upd.astype(BF16)
    rest = upd - high.astype(F32)
    mid = rest.astype(BF16)
    small = (rest - mid.astype(F32)).astype(BF16)
    moved = dot(high, perm, NT) + (dot(mid, perm, NT) + dot(small, perm, NT))
    igrad_ref[...] = og_ref[...].astype(F32) + moved

    for g in gathers:
        g.drain()
    s_a.drain(act_all)
    s_b.drain(act_all)
    rd_m().wait_send()
    for k in (1, 2):
        most = rd_pin.at[pl.ds(1, n - 1)]
        rd_copy(most, most, k, rd_recv_m.at[0], t.partner).wait_send()


def on_device(
    image_features,
    image_counts,
    slot_position,
    text_ids,
    norm_gain,
    norm_bias,
    proj_first,
    proj_second,
    embedding,
    rms_gain,
    gate_weight,
    up_weight,
    down_weight,
    output_grad,
):
    n = lax.axis_size("tensor_0")
    blocks = 2 * n * n
    seq, cols = output_grad.shape
    model = blocks * cols
    half = n // 2
    vmem = pl.BlockSpec(memory_space=pltpu.VMEM)
    smem = pl.BlockSpec(memory_space=pltpu.SMEM)
    hbm = pl.BlockSpec(memory_space=pl.ANY)
    dma = pltpu.SemaphoreType.DMA
    tile = (cols, LANES)
    hidden = gate_weight.shape[1]
    igrad, sgrad = pl.pallas_call(
        kernel_body,
        out_shape=(
            jax.ShapeDtypeStruct((cols, seq), F32),
            jax.ShapeDtypeStruct((cols, model), F32),
        ),
        in_specs=[
            vmem,
            smem,
            vmem,
            smem,
            vmem,
            vmem,
            hbm,
            hbm,
            hbm,
            vmem,
            hbm,
            hbm,
            hbm,
            vmem,
        ],
        out_specs=(vmem, vmem),
        scratch_shapes=[
            pltpu.VMEM(proj_first.shape, BF16),
            pltpu.VMEM(proj_second.shape, BF16),
            pltpu.VMEM((embedding.shape[1] // LANES, cols, LANES), BF16),
            pltpu.VMEM((model, 2 * hidden), BF16),
            pltpu.VMEM(down_weight.shape, BF16),
            pltpu.VMEM((2 * hidden, model), BF16),
            pltpu.VMEM((cols, blocks * LANES), BF16),
            pltpu.VMEM((blocks, LANES), F32),
            pltpu.VMEM((blocks, LANES), F32),
            pltpu.VMEM((LIVE, blocks * LANES), BF16),
            pltpu.VMEM((blocks, LIVE, LANES), BF16),
            pltpu.VMEM((blocks, *tile), BF16),
            pltpu.VMEM((blocks, cols, seq), BF16),
            pltpu.VMEM((blocks, *tile), BF16),
            pltpu.VMEM((blocks, *tile), BF16),
            pltpu.VMEM((cols, seq), BF16),
            pltpu.VMEM((2, blocks, *tile), F32),
            pltpu.VMEM((2, blocks // 2, *tile), BF16),
            pltpu.VMEM((2, blocks // 2, *tile), BF16),
            pltpu.VMEM((2, half, n, *tile), BF16),
            pltpu.VMEM((2, half, n, *tile), BF16),
            pltpu.VMEM((2, half, n, *tile), BF16),
            pltpu.VMEM((2, half, n, *tile), BF16),
            pltpu.VMEM((2, n, *tile), BF16),
            pltpu.VMEM((2, n, *tile), BF16),
            pltpu.VMEM((8, LANES), F32),
            pltpu.VMEM((8, LANES), F32),
            pltpu.VMEM((8, LANES), F32),
            pltpu.VMEM((n, 8, LANES), F32),
            pltpu.VMEM((8, LANES), F32),
            pltpu.VMEM((n, 8, LANES), F32),
            dma((6,)),
            dma((5, n)),
            dma((5, half, n)),
            dma((5, half, n)),
            dma((5, 1)),
            dma((5,)),
            dma((2, 1)),
            dma((2, 1)),
            dma((2, half, n)),
            dma((2, half, n)),
            dma((2, n)),
            dma((3,)),
            dma((n,)),
            dma((n,)),
            dma((1,)),
        ],
        compiler_params=pltpu.CompilerParams(
            collective_id=0, has_side_effects=True, vmem_limit_bytes=64 * 1024 * 1024 - 65536
        ),
        name="projector_step",
    )(
        image_features.T,
        image_counts,
        slot_position.reshape(1, -1),
        text_ids,
        norm_gain.reshape(1, -1),
        norm_bias.reshape(1, -1),
        proj_first,
        proj_second,
        embedding,
        rms_gain.reshape(1, -1),
        gate_weight,
        up_weight,
        down_weight,
        output_grad.T,
    )
    return igrad.T, sgrad


def solution(mesh):
    torus = Mesh(
        mesh.devices.reshape(mesh.shape["groups"], 8, 8, 2),
        ("groups", "tensor_0", "tensor_1", "tensor_2"),
    )
    in_specs = (
        P("groups", TENSOR),
        P("groups"),
        P("groups"),
        P("groups"),
        P(),
        P(),
        P(TENSOR, None),
        P(TENSOR, None),
        P(TENSOR, None),
        P(),
        P(None, TENSOR),
        P(None, TENSOR),
        P(TENSOR, None),
        P("groups", TENSOR),
    )
    out_specs = (P("groups", TENSOR), P(GROUPS_TENSOR, None))
    return jax.shard_map(
        on_device, mesh=torus, in_specs=in_specs, out_specs=out_specs, check_vma=False
    )
```

time: 531 us -> 141 us (0.27)
  waiting for transfers between devices: 255 us -> 0 us
  blocking collectives: 155 us -> 0 us
  Pallas kernels: 0 us -> 134 us
  local copies, waits for them, and re-layouts: 59.2 us -> 6.71 us
  matrix products: 24.4 us -> 0 us
  other arithmetic: 18 us -> 0 us
  between operations: 14.4 us -> 0.64 us
    reduce_scatter x3 -> x0, waiting for transfers between devices: 171 us -> none  [own_block(): parts = lax.psum_scatter(parts, axes[k], scatter_dimension=0, tiled=True)]
    pallas_call x0 -> x1, Pallas kernels: none -> 134 us  [on_device(): pl.pallas_call(kernel_body, out_shape=(jax.ShapeDtypeStruct((cols, seq),...]
    all_gather x3 -> x0, blocking collectives: 121 us -> none  [the longest x2 69.5 us: all_blocks(): parts = lax.all_gather(parts, axes[k])]
    all_gather x3 -> x0, waiting for transfers between devices: 82.8 us -> none  [the longest x1 78 us: on_device(): full_tokens = lax.all_gather(tokens, TENSOR, axis=1, tiled=True)]
    psum x3 -> x0, blocking collectives: 33.7 us -> none  [one_axis_at_a_time(): x = lax.psum(x, axis)]
    dot_general x7 -> x0, matrix products: 24.4 us -> none  [the longest x1 8.05 us: on_device(): lax.dot_general(gate_grad, gate_weight, (((1,), (1,)), ((), ())), preferr...]
    gather x5 -> x0, local copies, waits for them, and re-layouts: 12.1 us -> none  [the longest x1 8.23 us: on_device(): text_rows = jnp.take(embedding, text_ids, axis=1).T]
    unnamed x30 -> x2, local copies, waits for them, and re-layouts: 15.8 us -> 3.78 us
  transfers between devices with their start and end apart: 6 -> 0, of which waited for: 5 -> 0; matrix products, arithmetic and copies ran while one was open for 9% -> 0% of each run, Pallas kernels for 0% -> 0%
where the time goes in v1:
time: 141 us
  Pallas kernels  134 us (95%)
  local copies, waits for them, and re-layouts  6.71 us (5%)
    pallas_call x1, Pallas kernels, on_device(): pl.pallas_call(kernel_body, out_shape=(jax.ShapeDtypeStruct((cols, seq),...  134 us
    unnamed x2, local copies, waits for them, and re-layouts  3.78 us

profile of v1, /device:TPU:514, one launch (start us, length us, event | category | flops | bytes accessed | tf_op | source)
XLA Modules:
  0.0 141.1 jit_solution(11756830418055738542)
XLA Ops:
  0.6 1.5 %reshape.17.ngain_ref = f32[1,12800]{1,0:T(1,128)} reshape(f32[12800]{0:T(1024)} %param.18) | data formatting | bytes 102400 | tf_op jit(solution)/shard_map/reshape | solution.py:870
  2.1 1.5 %reshape.18.nbias_ref = f32[1,12800]{1,0:T(1,128)} reshape(f32[12800]{0:T(1024)} %param.19) | data formatting | bytes 102400 | tf_op jit(solution)/shard_map/reshape | solution.py:871
  3.6 133.8 %projector_step.1 = (f32[48,256]{1,0:T(8,128)}, f32[48,6144]{1,0:T(8,128)}) custom-call(bf16[100,128]{1,0:T(8,128)(2,1)} %bitcast.6, s32[2]{0:T(128)} %counts_ref.1, s32[1,128]{1,0:T(1,128)} %bitcast.9, s32[256]{0:T(256)} %ids_ref.1, f32[1,12800]{1,0:T(1,128)} %reshape.17.ngain_ref, f32[1,12800]{1,0:T(1,128)} %reshape.18.nbias_ref, ...), custom_call_target="tpu_custom_call" | custom-call | tf_op jit(solution)/shard_map/projector_step/pallas_call | solution.py:790
  137.3 1.4 %copy.18 = f32[256,48]{0,1:T(8,128)} copy(f32[256,48]{0,1:T(8,128)} %bitcast.5) | data formatting | bytes 98304
  138.7 2.4 %copy.19 = f32[48,6144]{1,0:T(8,128)} copy(f32[48,6144]{1,0:T(8,128)} %get-tuple-element.9) | data formatting | bytes 2359296

commit v2 on v1

v2 whole, which is shorter than its diff:
```python
import jax
import jax.numpy as jnp
from jax import lax
from jax.experimental import pallas as pl
from jax.experimental.pallas import tpu as pltpu
from jax.sharding import Mesh
from jax.sharding import PartitionSpec as P

LIVE = 80
TENSOR = ("tensor_0", "tensor_1", "tensor_2")
GROUPS_TENSOR = ("groups", "tensor_0", "tensor_1", "tensor_2")
MESH = pl.DeviceIdType.MESH
F32 = jnp.float32
BF16 = jnp.bfloat16
NT = (((1,), (1,)), ((), ()))
NN = (((1,), (0,)), ((), ()))
LANES = 128


def dot(a, b, dims=NN):
    return lax.dot_general(a, b, dims, preferred_element_type=F32)


def erf(x):
    x = jnp.clip(x, -3.832506856900711, 3.832506856900711)
    s = x * x
    top = jnp.full_like(x, 0.00022905065861350646)
    for k in (
        0.0034082910107109506,
        0.050955695062380861,
        0.18520832239976145,
        1.128379143519084,
    ):
        top = top * s + k
    low = jnp.full_like(x, -1.1791602954361697e-7)
    for k in (
        0.000023547966471313185,
        0.0010179625278914885,
        0.014070470171167667,
        0.11098505178285362,
        0.49746925110067538,
        1.0,
    ):
        low = low * s + k
    return x * top / low


class Torus:
    def __init__(self):
        self.c = lax.axis_index("tensor_2")
        self.x = lax.axis_index("tensor_0")
        self.y = lax.axis_index("tensor_1")
        self.n = lax.axis_size("tensor_0")
        self.p = self.pick(self.x, self.y)
        self.q = self.pick(self.y, self.x)
        self.me = self.block(self.p, self.q)
        self.partner = {"tensor_0": self.x, "tensor_1": self.y, "tensor_2": 1 - self.c}

    def pick(self, a, b):
        return (1 - self.c) * a + self.c * b

    def dev(self, p, q):
        return {"tensor_0": self.pick(p, q), "tensor_1": self.pick(q, p), "tensor_2": self.c}

    def chip(self, p, q):
        return self.pick(p, q) * self.n + self.pick(q, p)

    def block(self, p, q):
        return self.chip(p, q) * 2 + self.c

    def row(self, hop, down):
        last = self.n // 2 - 1
        return 2 * last if hop == last else hop + down * last

    def turn(self, a, d):
        return lax.rem(a + d + self.n, self.n)


class Gather:
    def __init__(self, t, buf, near, ring, mate, sent):
        self.t, self.buf = t, buf
        self.near, self.sems, self.mate, self.sent = near, ring, mate, sent

    def copy(self, j, dev, sem):
        return pltpu.make_async_remote_copy(
            self.buf.at[j], self.buf.at[j], self.sent, sem, device_id=dev, device_id_type=MESH
        )

    def to_mate(self, j):
        self.copy(j, self.t.partner, self.mate.at[0]).start()

    def got(self, j, sem):
        self.copy(j, self.t.partner, sem).wait_recv()

    def start(self):
        t = self.t

        @pl.loop(1, t.n)
        def _(d):
            self.copy(t.me, t.dev(t.turn(t.p, d), t.q), self.near.at[lax.div(d, 2)]).start()

        self.to_mate(t.me)

    def up(self, j, k, hop):
        t = self.t
        self.copy(j, t.dev(t.p, t.turn(t.q, 1)), self.sems.at[t.row(hop, 0), k]).start()

    def down(self, j, k, hop):
        t = self.t
        self.copy(j, t.dev(t.p, t.turn(t.q, -1)), self.sems.at[t.row(hop, 1), k]).start()

    def hop0(self):
        t = self.t

        def own(j, k):
            self.up(j, k, 0)
            self.down(j, k, 0)

        own(t.me, 0)
        j = t.block(t.turn(t.p, -1), t.q)
        self.got(j, self.near.at[0])
        own(j, 0)
        self.to_mate(j)

        @pl.loop(1, t.n // 2)
        def _(k):
            self.got(pl.ds(0, 2), self.near.at[k])
            for e in range(2):
                j = t.block(t.turn(t.p, -2 * k - e), t.q)
                own(j, k)
                self.to_mate(j)

    def hop(self, h):
        t = self.t
        half = t.n // 2
        few = half // 2

        def up(k, on):
            self.got(pl.ds(0, 2), self.sems.at[t.row(h - 1, 0), k])
            for e in range(2):
                j = t.block(t.turn(t.p, -2 * k - e), t.turn(t.q, -h))
                if on:
                    self.up(j, k, h)
                self.to_mate(j)

        def down(k, on):
            self.got(pl.ds(0, 2), self.sems.at[t.row(h - 1, 1), k])
            for e in range(2):
                j = t.block(t.turn(t.p, -2 * k - e), t.turn(t.q, h))
                if on:
                    self.down(j, k, h)
                self.to_mate(j)

        if h < half - 1:

            @pl.loop(0, half)
            def _(k):
                up(k, True)
                down(k, True)

        elif h == half - 1:

            @pl.loop(0, few)
            def _(k):
                up(k, True)
                down(k + few, True)
                down(k, False)
                up(k + few, False)

        else:

            @pl.loop(0, few)
            def _(k):
                up(k, False)
                down(k + few, False)

    def finish(self):
        half = self.buf.at[pl.ds(0, self.buf.shape[0] // 2)]
        pltpu.make_async_remote_copy(
            half, half, self.sent, self.mate.at[0], device_id=self.t.partner, device_id_type=MESH
        ).wait_recv()

    def drain(self):
        most = self.buf.at[pl.ds(0, self.buf.shape[0] - 1)]
        pltpu.make_async_remote_copy(
            most, most, self.sent, self.mate.at[0], device_id=self.t.partner, device_id_type=MESH
        ).wait_send()


class Leap(Gather):
    def send(self, j, k, far, dist, down):
        t = self.t
        by = -far if down else far
        sem = self.sems.at[t.row(dist - 1, down), k]
        self.copy(j, t.dev(t.p, t.turn(t.q, by)), sem).start()

    def hop0(self):
        t = self.t

        def own(j, k):
            for far in (2, 1):
                for down in (0, 1):
                    self.send(j, k, far, far, down)

        own(t.me, 0)
        j = t.block(t.turn(t.p, -1), t.q)
        self.got(j, self.near.at[0])
        own(j, 0)
        self.to_mate(j)

        @pl.loop(1, t.n // 2)
        def _(k):
            self.got(pl.ds(0, 2), self.near.at[k])
            for e in range(2):
                j = t.block(t.turn(t.p, -2 * k - e), t.q)
                own(j, k)
                self.to_mate(j)

    def arrived(self, k, dist, down, onward):
        t = self.t
        self.got(pl.ds(0, 2), self.sems.at[t.row(dist - 1, down), k])
        for e in range(2):
            by = dist if down else -dist
            j = t.block(t.turn(t.p, -2 * k - e), t.turn(t.q, by))
            for far in onward:
                self.send(j, k, far, dist + far, down)
            self.to_mate(j)

    def relay(self):
        few = self.t.n // 4

        @pl.loop(0, few)
        def _(k):
            self.arrived(k, 2, 0, (2, 1))
            self.arrived(k + few, 2, 1, (2, 1))

        @pl.loop(0, few)
        def _(k):
            self.arrived(k + few, 2, 0, (1,))
            self.arrived(k, 2, 1, (1,))

    def tail(self, dist):
        @pl.loop(0, self.t.n // 2)
        def _(k):
            self.arrived(k, dist, 0, ())
            self.arrived(k, dist, 1, ())

    def tail4(self):
        few = self.t.n // 4

        @pl.loop(0, few)
        def _(k):
            self.arrived(k, 4, 0, ())
            self.arrived(k + few, 4, 1, ())


class Scatter:
    def __init__(self, t, part, give, take, out_up, out_dn, in_up, in_dn, fin_out, fin_in, sems):
        self.t, self.part, self.give, self.take = t, part, give, take
        self.out_up, self.out_dn, self.in_up, self.in_dn = out_up, out_dn, in_up, in_dn
        self.fin_out, self.fin_in = fin_out, fin_in
        self.sent, self.mate, self.ring, self.near = sems

    def mate_copy(self, span):
        return pltpu.make_async_remote_copy(
            self.give.at[span],
            self.take.at[span],
            self.sent.at[0],
            self.mate.at[0],
            device_id=self.t.partner,
            device_id_type=MESH,
        )

    def fill(self, k, even, odd):
        span = pl.ds(k * even.shape[0], even.shape[0])
        self.part[span] = jnp.where(self.t.c == 0, even, odd)
        self.give[span] = jnp.where(self.t.c == 0, odd, even).astype(BF16)
        self.mate_copy(span).start()

    def mated(self):
        self.mate_copy(pl.ds(0, self.give.shape[0])).wait_recv()

    def base(self, p, q):
        t = self.t
        i = t.chip(p, q)
        return self.part[i] + self.take[i].astype(F32)

    def ring_copy(self, dist, d, down):
        t = self.t
        hop = dist if dist < 3 else dist - 2
        out, into = (self.out_dn, self.in_dn) if down else (self.out_up, self.in_up)
        return pltpu.make_async_remote_copy(
            out.at[dist - 1, d],
            into.at[dist - 1, d],
            self.sent.at[0],
            self.ring.at[t.row(dist - 1, down), lax.div(d, 2)],
            device_id=t.dev(t.p, t.turn(t.q, -hop if down else hop)),
            device_id_type=MESH,
        )

    def pair(self, dist, k, down):
        two = (self.in_dn if down else self.in_up).at[dist - 1, pl.ds(2 * k, 2)]
        pltpu.make_async_remote_copy(
            two,
            two,
            self.sent.at[0],
            self.ring.at[self.t.row(dist - 1, down), k],
            device_id=self.t.partner,
            device_id_type=MESH,
        ).wait_recv()

    def send(self, dist, k, down, had):
        t = self.t
        into = self.in_dn if down else self.in_up
        out = self.out_dn if down else self.out_up
        for h in had:
            self.pair(h, k, down)
        for e in range(2):
            d = 2 * k + e
            value = self.base(t.turn(t.p, -d), t.turn(t.q, -dist if down else dist))
            for h in had:
                value = value + into[h - 1, d].astype(F32)
            out[dist - 1, d] = value.astype(BF16)
            self.ring_copy(dist, d, down).start()

    def stage1(self):
        few = self.t.n // 4

        @pl.loop(0, few)
        def _(k):
            self.send(4, k, 0, ())
            self.send(4, k + few, 1, ())

        @pl.loop(0, 2 * few)
        def _(k):
            self.send(3, k, 0, ())
            self.send(3, k, 1, ())

    def stage1b(self):
        @pl.loop(0, self.t.n // 2)
        def _(k):
            self.send(1, k, 0, ())
            self.send(1, k, 1, ())

    def stage2(self):
        few = self.t.n // 4

        @pl.loop(0, few)
        def _(k):
            self.send(2, k, 0, (3, 4))
            self.send(2, k + few, 1, (3, 4))
            self.send(2, k + few, 0, (3,))
            self.send(2, k, 1, (3,))

    def fin_copy(self, d):
        t = self.t
        return pltpu.make_async_remote_copy(
            self.fin_out.at[d],
            self.fin_in.at[d],
            self.sent.at[0],
            self.near.at[lax.div(d, 2)],
            device_id=t.dev(t.turn(t.p, -d), t.q),
            device_id_type=MESH,
        )

    def whole(self, d):
        value = self.base(self.t.turn(self.t.p, -d), self.t.q)
        for into in (self.in_up, self.in_dn):
            for dist in (1, 2):
                value = value + into[dist - 1, d].astype(F32)
        return value

    def last(self):
        t = self.t

        def both(k):
            for down in (0, 1):
                for dist in (1, 2):
                    self.pair(dist, k, down)

        def give(d):
            self.fin_out[d] = self.whole(d).astype(BF16)
            self.fin_copy(d).start()

        both(0)
        give(1)

        @pl.loop(1, t.n // 2)
        def _(k):
            both(k)
            give(2 * k)
            give(2 * k + 1)

        return self.whole(0)

    def collect(self, value):
        self.fin_copy(1).wait_recv()
        value = value + self.fin_in[1].astype(F32)
        for k in range(1, self.t.n // 2):
            two = self.fin_in.at[pl.ds(2 * k, 2)]
            pltpu.make_async_remote_copy(
                two,
                two,
                self.sent.at[0],
                self.near.at[k],
                device_id=self.t.partner,
                device_id_type=MESH,
            ).wait_recv()
            value = value + self.fin_in[2 * k].astype(F32) + self.fin_in[2 * k + 1].astype(F32)
        return value

    def drain(self, like):
        most = like.at[pl.ds(0, like.shape[0] - 1)]
        pltpu.make_async_remote_copy(
            most, most, self.sent.at[0], self.mate.at[0], device_id=self.t.partner, device_id_type=MESH
        ).wait_send()


def kernel_body(
    feats_ref,
    counts_ref,
    pos_ref,
    ids_ref,
    ngain_ref,
    nbias_ref,
    first_hbm,
    second_hbm,
    emb_hbm,
    rgain_ref,
    gate_hbm,
    up_hbm,
    down_hbm,
    og_ref,
    igrad_ref,
    pgrad_ref,
    act_hbm,
    first_v,
    second_v,
    emb_v,
    wcat,
    down_v,
    wt,
    wpad,
    gb_ref,
    feats_all,
    act_all,
    og_all,
    ta_all,
    tb_all,
    text_own,
    part,
    give,
    take,
    out_up,
    out_dn,
    in_up,
    in_dn,
    fin_out,
    fin_in,
    rd_own,
    rd_mate,
    rd_p,
    rd_pin,
    rd_q,
    rd_qin,
    load_sem,
    near_sem,
    ring_sem,
    mate_sem,
    sent_sem,
    rs_sent,
    rs_mate,
    rd_sent,
    rd_recv_p,
    rd_recv_q,
    rd_recv_m,
):
    t = Torus()
    n = t.n
    blocks = 2 * n * n
    cols, seq = og_ref.shape
    width, slots = feats_ref.shape
    model = blocks * cols
    pix = blocks * width

    barrier = pltpu.get_barrier_semaphore()

    @pl.loop(1, n)
    def _(d):
        pl.semaphore_signal(
            barrier, inc=1, device_id=t.dev(t.turn(t.p, d), t.q), device_id_type=MESH
        )
        pl.semaphore_signal(
            barrier, inc=1, device_id=t.dev(t.p, t.turn(t.q, d)), device_id_type=MESH
        )

    pl.semaphore_signal(barrier, inc=1, device_id=t.partner, device_id_type=MESH)

    loads = [
        pltpu.make_async_copy(first_hbm, first_v, load_sem.at[0]),
        pltpu.make_async_copy(gate_hbm, wcat.at[:, pl.ds(0, LANES)], load_sem.at[1]),
        pltpu.make_async_copy(up_hbm, wcat.at[:, pl.ds(LANES, LANES)], load_sem.at[2]),
        pltpu.make_async_copy(second_hbm, second_v, load_sem.at[3]),
        pltpu.make_async_copy(down_hbm, down_v, load_sem.at[4]),
    ]
    loads[0].start()

    slot = lax.broadcasted_iota(jnp.int32, (LIVE, slots), 1)
    row = lax.broadcasted_iota(jnp.int32, (LIVE, slots), 0)
    images = counts_ref.shape[0]
    per = slots // images
    at = slot % per
    live = jnp.zeros((LIVE, slots), jnp.int32)
    rank = at
    before = 0
    for k in range(images):
        count = counts_ref[k]
        here = (slot // per) == k
        live = jnp.where(here & (at < count), 1, live)
        rank = jnp.where(here, at + before, rank)
        before = before + count
    choose = jnp.where((live == 1) & (rank == row), 1.0, 0.0).astype(BF16)
    feats_own = dot(choose, feats_ref[...], NT)
    feats_all[t.me] = jnp.zeros((LIVE, LANES), BF16)
    feats_all[t.me, :, 0:width] = feats_own.astype(BF16)

    gathers = []
    for k, buf in enumerate((feats_all, og_all, ta_all, act_all, tb_all)):
        kind = Leap if k > 2 else Gather
        gathers.append(
            kind(t, buf, near_sem.at[k], ring_sem.at[k], mate_sem.at[k], sent_sem.at[k])
        )
    g_feats, g_og, g_ta, g_act, g_tb = gathers

    pl.semaphore_wait(barrier, 2 * (n - 1) + 1)
    g_feats.start()

    @pl.loop(0, emb_v.shape[0], unroll=8)
    def _(k):
        span = pl.ds(pl.multiple_of(k * LANES, LANES), LANES)
        pltpu.make_async_copy(emb_hbm.at[:, span], emb_v.at[k], load_sem.at[5]).start()

    for load in loads[1:]:
        load.start()

    pos = pos_ref[...]
    where_row = lax.broadcasted_iota(jnp.int32, (seq, slots), 0)
    hit = jnp.where((where_row == pos) & (live[0:1] == 1), 1.0, 0.0)
    is_img = jnp.sum(hit, axis=1, keepdims=True)
    img_rank = jnp.sum(hit * rank[0:1].astype(F32), axis=1, keepdims=True)
    low = jnp.where(
        lax.broadcasted_iota(jnp.int32, (seq, seq), 1)
        < lax.broadcasted_iota(jnp.int32, (seq, seq), 0),
        1.0,
        0.0,
    ).astype(BF16)
    not_img = jnp.broadcast_to(1.0 - is_img, (seq, LANES)).astype(BF16)
    text_rank = dot(low, not_img)[:, 0:1]
    text_col = jnp.where(text_rank < LANES, text_rank, text_rank + LIVE)
    col_of = jnp.where(is_img > 0.5, LANES + img_rank, text_col)
    perm = jnp.where(
        lax.broadcasted_iota(jnp.int32, (seq, seq), 1).astype(F32) == col_of, 1.0, 0.0
    ).astype(BF16)
    og_packed = dot(og_ref[...], perm).astype(BF16)
    og_all[t.me] = og_packed
    g_og.start()

    loads[0].wait()
    wpad[...] = jnp.zeros(wpad.shape, BF16)
    gb_ref[...] = jnp.zeros(gb_ref.shape, F32)
    for j in range(blocks):
        wpad[:, LANES * j : LANES * j + width] = first_v[:, width * j : width * (j + 1)]
        line, start = divmod(width * j, LANES)
        fit = min(width, LANES - start)
        for k, ref in enumerate((ngain_ref, nbias_ref)):
            gb_ref[k, j : j + 1, 0:fit] = ref[line : line + 1, start : start + fit]
            if fit < width:
                gb_ref[k, j : j + 1, fit:width] = ref[line + 1 : line + 2, 0 : width - fit]

    pltpu.make_async_copy(emb_v, emb_v, load_sem.at[5]).wait()
    lane = lax.broadcasted_iota(jnp.int32, (cols, LANES), 1)

    def embed(tile):
        def one(k, acc):
            word = ids_ref[tile * LANES + k]
            inside = lax.rem(word, LANES)
            found = emb_v[lax.div(word, LANES)].astype(F32)
            column = jnp.sum(jnp.where(lane == inside, found, 0.0), axis=1, keepdims=True)
            return jnp.where(lane == k, column, acc)

        text_own[:, pl.ds(tile * LANES, LANES)] = lax.fori_loop(
            0, LANES, one, jnp.zeros((cols, LANES), F32), unroll=8
        ).astype(BF16)

    embed(0)
    embed(1)
    text_packed = dot(text_own[...], perm)
    text_a = text_packed[:, 0:LANES]
    text_b_tile = text_packed[:, LANES : 2 * LANES]
    ta_all[t.me] = text_a.astype(BF16)
    g_ta.start()

    g_feats.hop0()
    g_feats.hop(1)
    g_feats.hop(2)
    g_feats.hop(3)
    g_og.hop0()
    g_feats.hop(4)

    shift = feats_all[t.me].astype(F32)[:, 0:1]

    band = 16
    bands = LIVE // band

    def sums_of(core, carry):
        out = []
        for r in range(bands):
            rows = pl.ds(r * band, band)
            about = jnp.broadcast_to(shift[r * band : (r + 1) * band], (band, LANES))

            def add_up(k, pair):
                moved = feats_all[2 * k + core, rows].astype(F32) - about
                return pair[0] + moved, pair[1] + moved * moved

            out.append(lax.fori_loop(0, blocks // 2, add_up, carry[r], unroll=8))
        return out

    zero = jnp.zeros((band, LANES), F32)
    sums = sums_of(t.c, [(zero, zero)] * bands)
    g_feats.finish()
    sums = sums_of(1 - t.c, sums)
    sums = [jnp.concatenate([sums[r][e] for r in range(bands)], axis=0) for e in range(2)]
    inside = lax.broadcasted_iota(jnp.int32, (LIVE, LANES), 1) < width
    off = jnp.sum(jnp.where(inside, sums[0], 0.0), axis=1, keepdims=True) / pix
    square = jnp.sum(jnp.where(inside, sums[1], 0.0), axis=1, keepdims=True) / pix
    mean = shift + off
    scale = lax.rsqrt(jnp.maximum(square - off * off, 0.0) + 1e-05)
    g_og.hop(1)
    g_ta.hop0()

    fold = 8

    def first_step(k, acc):
        tiles = []
        for e in range(fold):
            j = k * fold + e
            centre = feats_all[j].astype(F32) - mean
            value = centre * scale * gb_ref[0, pl.ds(j, 1), :] + gb_ref[1, pl.ds(j, 1), :]
            tiles.append(value.astype(BF16))
        span = pl.ds(pl.multiple_of(k * fold * LANES, fold * LANES), fold * LANES)
        return acc + dot(wpad[:, span], jnp.concatenate(tiles, axis=1), NT)

    hidden = lax.fori_loop(
        0, blocks // fold, first_step, jnp.zeros((cols, LIVE), F32), unroll=2
    )
    hidden = 0.5 * hidden * (1.0 + erf(hidden * 0.7071067811865476))
    act_all[t.me] = jnp.zeros((cols, LANES), BF16)
    act_all[t.me, :, 0:LIVE] = hidden.astype(BF16)
    g_act.start()

    loads[1].wait()
    loads[2].wait()
    big_eye = jnp.where(
        lax.broadcasted_iota(jnp.int32, (seq, seq), 1)
        == lax.broadcasted_iota(jnp.int32, (seq, seq), 0),
        1.0,
        0.0,
    ).astype(BF16)

    def turn_weights(a, b):
        @pl.loop(a, b, unroll=2)
        def _(k):
            at_row = pl.multiple_of(k * seq, seq)
            flipped = dot(big_eye, wcat[pl.ds(at_row, seq), :], NT)
            wt[:, pl.ds(at_row, seq)] = (flipped * rgain_ref[:, pl.ds(at_row, seq)]).astype(BF16)

    pieces = model // seq
    cut = [pieces * k // 6 for k in range(7)]
    g_og.hop(2)
    turn_weights(cut[0], cut[1])
    g_ta.hop(1)
    turn_weights(cut[1], cut[2])
    g_act.hop0()
    g_og.hop(3)
    turn_weights(cut[2], cut[3])
    g_ta.hop(2)
    turn_weights(cut[3], cut[4])
    g_act.relay()
    g_act.tail(1)
    g_ta.hop(3)
    turn_weights(cut[4], cut[5])
    g_og.hop(4)
    turn_weights(cut[5], cut[6])
    g_act.tail(3)
    g_act.tail4()
    g_act.finish()
    keep = pltpu.make_async_copy(act_all, act_hbm, load_sem.at[6])
    keep.start()

    loads[3].wait()
    group = blocks // 8
    span_rows = group * cols

    def rows_of(buf, k):
        return buf[pl.ds(k * group, group)].reshape(span_rows, buf.shape[2])

    def second_step(k, acc):
        span = pl.ds(pl.multiple_of(k * span_rows, span_rows), span_rows)
        return acc + dot(second_v[:, span], rows_of(act_all, k))

    projected = lax.fori_loop(0, 8, second_step, jnp.zeros((cols, LANES), F32), unroll=8)
    tb_all[t.me] = jnp.where(lane < LIVE, projected, text_b_tile).astype(BF16)
    g_tb.start()

    g_ta.hop(4)
    g_og.finish()
    loads[4].wait()

    def down_step(k, acc):
        span = pl.ds(pl.multiple_of(k * span_rows, span_rows), span_rows)
        return acc + dot(down_v[:, span], rows_of(og_all, k))

    hidden_grad = lax.fori_loop(0, 8, down_step, jnp.zeros((LANES, seq), F32), unroll=4)
    scatters = []
    for k, share in enumerate((0, 3)):
        scatters.append(
            Scatter(
                t,
                part.at[k],
                give.at[k],
                take.at[k],
                out_up.at[k],
                out_dn.at[k],
                in_up.at[k],
                in_dn.at[k],
                fin_out.at[k],
                fin_in.at[k],
                (rs_sent.at[k], rs_mate.at[k], ring_sem.at[share], near_sem.at[share]),
            )
        )
    s_a, s_b = scatters

    def gates(buf, hid):
        def step(k, carry):
            acc, sq = carry
            rows = rows_of(buf, k)
            span = pl.ds(pl.multiple_of(k * span_rows, span_rows), span_rows)
            wide = rows.astype(F32)
            sq = sq + jnp.sum(wide * wide, axis=0, keepdims=True)
            return acc + dot(wt[:, span], rows), sq

        acc, sq = lax.fori_loop(
            0,
            8,
            step,
            (jnp.zeros((2 * LANES, LANES), F32), jnp.zeros((1, LANES), F32)),
            unroll=4,
        )
        inv = lax.rsqrt(sq / model + 1e-05)
        acc = acc * inv
        gate, up = acc[0:LANES], acc[LANES : 2 * LANES]
        sig = 1.0 / (1.0 + jnp.exp(-gate))
        gate_grad = (hid * up * sig * (1.0 + gate * (1.0 - sig))).astype(BF16)
        up_grad = (hid * gate * sig).astype(BF16)
        dots = jnp.sum(
            gate_grad.astype(F32) * gate + up_grad.astype(F32) * up, axis=0, keepdims=True
        )
        both = jnp.concatenate([gate_grad, up_grad], axis=0)

        return inv, dots, both

    def spread_out(both, scatter):
        @pl.loop(0, 8, unroll=2)
        def _(k):
            at_row = pl.multiple_of(k * span_rows, span_rows)
            value = dot(wcat[pl.ds(at_row, span_rows), :], both)
            value = value.reshape(group // 2, 2, cols, LANES)
            scatter.fill(k, value[:, 0], value[:, 1])

    g_ta.finish()
    inv_a, dots_a, both_a = gates(ta_all, hidden_grad[:, 0:LANES])
    g_tb.hop0()
    spread_out(both_a, s_a)
    g_tb.relay()
    s_a.mated()
    s_a.stage1()
    g_tb.tail(1)
    s_a.stage1b()
    g_tb.tail(3)
    g_tb.tail4()
    g_tb.finish()
    inv_b, dots_b, both_b = gates(tb_all, hidden_grad[:, LANES : 2 * LANES])
    s_a.stage2()
    spread_out(both_b, s_b)

    rd_own[...] = jnp.zeros(rd_own.shape, F32)
    rd_own[0:1] = dots_a
    rd_own[1:2] = dots_b

    def rd_copy(src, dst, sem_at, recv, dev):
        return pltpu.make_async_remote_copy(
            src, dst, rd_sent.at[sem_at], recv, device_id=dev, device_id_type=MESH
        )

    def rd_m():
        return rd_copy(rd_own, rd_mate, 0, rd_recv_m.at[0], t.partner)

    def rd_along_p(d):
        return rd_copy(rd_p, rd_pin.at[d], 1, rd_recv_p.at[d], t.dev(t.turn(t.p, d), t.q))

    def rd_along_q(d):
        return rd_copy(rd_q, rd_qin.at[d], 2, rd_recv_q.at[d], t.dev(t.p, t.turn(t.q, d)))

    rd_m().start()
    s_b.mated()
    s_b.stage1()
    rd_m().wait_recv()
    rd_p[...] = rd_own[...] + rd_mate[...]

    @pl.loop(1, n)
    def _(d):
        rd_along_p(d).start()

    s_b.stage1b()
    sum_a = s_a.last()
    s_b.stage2()
    rd_sum = rd_p[...]
    for d in range(1, n):
        rd_along_p(d).wait_recv()
        rd_sum = rd_sum + rd_pin[d]
    rd_q[...] = rd_sum

    @pl.loop(1, n)
    def _(d):
        rd_along_q(d).start()

    own = lax.broadcasted_iota(jnp.int32, (cols, model), 1) == (
        lax.broadcasted_iota(jnp.int32, (cols, model), 0) + t.me * cols
    )
    gain_own = jnp.sum(jnp.where(own, rgain_ref[...], 0.0), axis=1, keepdims=True)
    sum_b = s_b.last()
    grad_a = s_a.collect(sum_a)
    rd_all = rd_q[...]
    for d in range(1, n):
        rd_along_q(d).wait_recv()
        rd_all = rd_all + rd_qin[d]
    grad_b = s_b.collect(sum_b)

    def update(grad, tokens, inv, dots):
        unit = tokens.astype(F32) * inv
        return inv * (gain_own * grad - unit * (dots / model))

    upd_a = update(grad_a, ta_all[t.me], inv_a, rd_all[0:1])
    upd_b = update(grad_b, tb_all[t.me], inv_b, rd_all[1:2])
    grad_img = og_all[t.me, :, LANES : 2 * LANES].astype(F32) + upd_b
    proj_grad = jnp.where(lane < LIVE, grad_img, 0.0).astype(BF16)

    pgrad_ref[...] = proj_grad

    upd = jnp.concatenate([upd_a, upd_b], axis=1)
    high = upd.astype(BF16)
    rest = upd - high.astype(F32)
    mid = rest.astype(BF16)
    small = (rest - mid.astype(F32)).astype(BF16)
    moved = dot(high, perm, NT) + (dot(mid, perm, NT) + dot(small, perm, NT))
    igrad_ref[...] = og_ref[...].astype(F32) + moved

    keep.wait()
    for g in gathers:
        g.drain()
    s_a.drain(act_all)
    s_b.drain(act_all)
    rd_m().wait_send()
    for k in (1, 2):
        most = rd_pin.at[pl.ds(1, n - 1)]
        rd_copy(most, most, k, rd_recv_m.at[0], t.partner).wait_send()


def second_grad_body(pgrad_ref, act_ref, igrad_in, sgrad_ref, igrad_out):
    sgrad_ref[...] = dot(pgrad_ref[...], act_ref[...], NT)

    @pl.when(pl.program_id(0) == 0)
    def _():
        igrad_out[...] = igrad_in[...]


def on_device(
    image_features,
    image_counts,
    slot_position,
    text_ids,
    norm_gain,
    norm_bias,
    proj_first,
    proj_second,
    embedding,
    rms_gain,
    gate_weight,
    up_weight,
    down_weight,
    output_grad,
):
    n = lax.axis_size("tensor_0")
    blocks = 2 * n * n
    seq, cols = output_grad.shape
    model = blocks * cols
    half = n // 2
    vmem = pl.BlockSpec(memory_space=pltpu.VMEM)
    smem = pl.BlockSpec(memory_space=pltpu.SMEM)
    hbm = pl.BlockSpec(memory_space=pl.ANY)
    dma = pltpu.SemaphoreType.DMA
    tile = (cols, LANES)
    hidden = gate_weight.shape[1]
    igrad, pgrad, act = pl.pallas_call(
        kernel_body,
        out_shape=(
            jax.ShapeDtypeStruct((cols, seq), F32),
            jax.ShapeDtypeStruct((cols, LANES), BF16),
            jax.ShapeDtypeStruct((blocks, *tile), BF16),
        ),
        in_specs=[
            vmem,
            smem,
            vmem,
            smem,
            vmem,
            vmem,
            hbm,
            hbm,
            hbm,
            vmem,
            hbm,
            hbm,
            hbm,
            vmem,
        ],
        out_specs=(vmem, vmem, hbm),
        scratch_shapes=[
            pltpu.VMEM(proj_first.shape, BF16),
            pltpu.VMEM(proj_second.shape, BF16),
            pltpu.VMEM((embedding.shape[1] // LANES, cols, LANES), BF16),
            pltpu.VMEM((model, 2 * hidden), BF16),
            pltpu.VMEM(down_weight.shape, BF16),
            pltpu.VMEM((2 * hidden, model), BF16),
            pltpu.VMEM((cols, blocks * LANES), BF16),
            pltpu.VMEM((2, blocks, LANES), F32),
            pltpu.VMEM((blocks, LIVE, LANES), BF16),
            pltpu.VMEM((blocks, *tile), BF16),
            pltpu.VMEM((blocks, cols, seq), BF16),
            pltpu.VMEM((blocks, *tile), BF16),
            pltpu.VMEM((blocks, *tile), BF16),
            pltpu.VMEM((cols, seq), BF16),
            pltpu.VMEM((2, blocks // 2, *tile), F32),
            pltpu.VMEM((2, blocks // 2, *tile), BF16),
            pltpu.VMEM((2, blocks // 2, *tile), BF16),
            pltpu.VMEM((2, half, n, *tile), BF16),
            pltpu.VMEM((2, half, n, *tile), BF16),
            pltpu.VMEM((2, half, n, *tile), BF16),
            pltpu.VMEM((2, half, n, *tile), BF16),
            pltpu.VMEM((2, n, *tile), BF16),
            pltpu.VMEM((2, n, *tile), BF16),
            pltpu.VMEM((8, LANES), F32),
            pltpu.VMEM((8, LANES), F32),
            pltpu.VMEM((8, LANES), F32),
            pltpu.VMEM((n, 8, LANES), F32),
            pltpu.VMEM((8, LANES), F32),
            pltpu.VMEM((n, 8, LANES), F32),
            dma((7,)),
            dma((5, half)),
            dma((5, n - 1, half)),
            dma((5, 1)),
            dma((5,)),
            dma((2, 1)),
            dma((2, 1)),
            dma((3,)),
            dma((n,)),
            dma((n,)),
            dma((1,)),
        ],
        compiler_params=pltpu.CompilerParams(
            collective_id=0, has_side_effects=True, vmem_limit_bytes=64 * 1024 * 1024 - 65536
        ),
        name="projector_step",
    )(
        image_features.T,
        image_counts,
        slot_position.reshape(1, -1),
        text_ids,
        norm_gain.reshape(-1, LANES),
        norm_bias.reshape(-1, LANES),
        proj_first,
        proj_second,
        embedding,
        rms_gain.reshape(1, -1),
        gate_weight,
        up_weight,
        down_weight,
        output_grad.T,
    )
    parts = 2
    sgrad, igrad = pl.pallas_call(
        second_grad_body,
        grid=(parts,),
        out_shape=(
            jax.ShapeDtypeStruct((cols, model), F32),
            jax.ShapeDtypeStruct((cols, seq), F32),
        ),
        in_specs=[
            pl.BlockSpec(tile, lambda k: (0, 0)),
            pl.BlockSpec((model // parts, LANES), lambda k: (k, 0)),
            pl.BlockSpec((cols, seq), lambda k: (0, 0)),
        ],
        out_specs=(
            pl.BlockSpec((cols, model // parts), lambda k: (0, k)),
            pl.BlockSpec((cols, seq), lambda k: (0, 0)),
        ),
        name="second_grad",
    )(pgrad, act.reshape(model, LANES), igrad)
    return igrad.T, sgrad


def solution(mesh):
    torus = Mesh(
        mesh.devices.reshape(mesh.shape["groups"], 8, 8, 2),
        ("groups", "tensor_0", "tensor_1", "tensor_2"),
    )
    in_specs = (
        P("groups", TENSOR),
        P("groups"),
        P("groups"),
        P("groups"),
        P(),
        P(),
        P(TENSOR, None),
        P(TENSOR, None),
        P(TENSOR, None),
        P(),
        P(None, TENSOR),
        P(None, TENSOR),
        P(TENSOR, None),
        P("groups", TENSOR),
    )
    out_specs = (P("groups", TENSOR), P(GROUPS_TENSOR, None))
    return jax.shard_map(
        on_device, mesh=torus, in_specs=in_specs, out_specs=out_specs, check_vma=False
    )
```

time: 141 us -> 111 us (0.79)
  Pallas kernels: 134 us -> 110 us
  local copies, waits for them, and re-layouts: 6.71 us -> 0 us
    pallas_call x1, Pallas kernels: 134 us -> 107 us  [on_device(): pl.pallas_call(kernel_body, out_shape=(jax.ShapeDtypeStruct((cols, seq),...]
    unnamed x2 -> x0, local copies, waits for them, and re-layouts: 3.78 us -> none
    reshape x2 -> x0, local copies, waits for them, and re-layouts: 2.93 us -> none  [the longest x1 1.47 us: on_device(): norm_bias.reshape(1, -1)]
    pallas_call x0 -> x1, Pallas kernels: none -> 2.74 us  [on_device(): pl.pallas_call(second_grad_body, grid=(parts,), out_shape=(jax.ShapeDtype...]
where the time goes in v2:
time: 111 us; the launch traced here: 110 us
  Pallas kernels  110 us (99%)
    pallas_call x1, Pallas kernels, on_device(): pl.pallas_call(kernel_body, out_shape=(jax.ShapeDtypeStruct((cols, seq),...  107 us
    pallas_call x1, Pallas kernels, on_device(): pl.pallas_call(second_grad_body, grid=(parts,), out_shape=(jax.ShapeDtype...  2.74 us

profile of v2, /device:TPU:514, one launch (start us, length us, event | category | flops | bytes accessed | tf_op | source)
XLA Modules:
  0.0 110.4 jit_solution(6604289213380212632)
XLA Ops:
  0.6 107.0 %projector_step.1 = (f32[48,256]{1,0:T(8,128)}, bf16[48,128]{1,0:T(8,128)(2,1)}, bf16[128,48,128]{2,1,0:T(8,128)(2,1)}) custom-call(bf16[100,128]{1,0:T(8,128)(2,1)} %bitcast.11, s32[2]{0:T(128)} %counts_ref.1, s32[1,128]{1,0:T(1,128)} %bitcast.14, s32[256]{0:T(256)} %ids_ref.1, f32[100,128]{1,0:T(8,128)} %bitcast.9, f32[100,128]{1,0:T(8,128)} %bitcast.10, ...), custom_call_target="tpu_custom_call" | custom-call | tf_op jit(solution)/shard_map/projector_step/pallas_call | solution.py:914
  107.7 2.7 %second_grad.1 = (f32[48,6144]{1,0:T(8,128)}, f32[48,256]{1,0:T(8,128)}) custom-call(bf16[48,128]{1,0:T(8,128)(2,1)} %get-tuple-element.7.pgrad_ref, bf16[6144,128]{1,0:T(8,128)(2,1)} %bitcast.8, f32[48,256]{1,0:T(8,128)} %get-tuple-element.9.igrad_in), custom_call_target="tpu_custom_call" | custom-call | tf_op jit(solution)/shard_map/second_grad/pallas_call | solution.py:1001

commit v3 on v2

--- a/solution.py
+++ b/solution.py
@@ -417,23 +417,31 @@
 
 
 def kernel_body(
+    feats_hbm,
+    counts_hbm,
+    pos_hbm,
+    ids_hbm,
+    ngain_hbm,
+    nbias_hbm,
+    first_hbm,
+    second_hbm,
+    emb_hbm,
+    rgain_hbm,
+    gate_hbm,
+    up_hbm,
+    down_hbm,
+    og_hbm,
+    igrad_ref,
+    pgrad_ref,
+    act_hbm,
     feats_ref,
     counts_ref,
     pos_ref,
     ids_ref,
     ngain_ref,
     nbias_ref,
-    first_hbm,
-    second_hbm,
-    emb_hbm,
     rgain_ref,
-    gate_hbm,
-    up_hbm,
-    down_hbm,
     og_ref,
-    igrad_ref,
-    pgrad_ref,
-    act_hbm,
     first_v,
     second_v,
     emb_v,
@@ -464,6 +472,7 @@
     rd_q,
     rd_qin,
     load_sem,
+    small_sem,
     near_sem,
     ring_sem,
     mate_sem,
@@ -503,7 +512,26 @@
         pltpu.make_async_copy(second_hbm, second_v, load_sem.at[3]),
         pltpu.make_async_copy(down_hbm, down_v, load_sem.at[4]),
     ]
+    smalls = [
+        pltpu.make_async_copy(src, dst, small_sem.at[k])
+        for k, (src, dst) in enumerate(
+            (
+                (feats_hbm, feats_ref),
+                (counts_hbm, counts_ref),
+                (pos_hbm, pos_ref),
+                (ids_hbm, ids_ref),
+                (ngain_hbm, ngain_ref),
+                (nbias_hbm, nbias_ref),
+                (rgain_hbm, rgain_ref),
+                (og_hbm, og_ref),
+            )
+        )
+    ]
+    for small in smalls:
+        small.start()
     loads[0].start()
+    smalls[0].wait()
+    smalls[1].wait()
 
     slot = lax.broadcasted_iota(jnp.int32, (LIVE, slots), 1)
     row = lax.broadcasted_iota(jnp.int32, (LIVE, slots), 0)
@@ -526,7 +554,7 @@
 
     gathers = []
     for k, buf in enumerate((feats_all, og_all, ta_all, act_all, tb_all)):
-        kind = Leap if k > 2 else Gather
+        kind = Gather if k in (1, 2) else Leap
         gathers.append(
             kind(t, buf, near_sem.at[k], ring_sem.at[k], mate_sem.at[k], sent_sem.at[k])
         )
@@ -543,6 +571,8 @@
     for load in loads[1:]:
         load.start()
 
+    smalls[2].wait()
+    smalls[7].wait()
     pos = pos_ref[...]
     where_row = lax.broadcasted_iota(jnp.int32, (seq, slots), 0)
     hit = jnp.where((where_row == pos) & (live[0:1] == 1), 1.0, 0.0)
@@ -566,6 +596,8 @@
     g_og.start()
 
     loads[0].wait()
+    smalls[4].wait()
+    smalls[5].wait()
     wpad[...] = jnp.zeros(wpad.shape, BF16)
     gb_ref[...] = jnp.zeros(gb_ref.shape, F32)
     for j in range(blocks):
@@ -578,6 +610,7 @@
                 gb_ref[k, j : j + 1, fit:width] = ref[line + 1 : line + 2, 0 : width - fit]
 
     pltpu.make_async_copy(emb_v, emb_v, load_sem.at[5]).wait()
+    smalls[3].wait()
     lane = lax.broadcasted_iota(jnp.int32, (cols, LANES), 1)
 
     def embed(tile):
@@ -593,42 +626,51 @@
         ).astype(BF16)
 
     embed(0)
+
+    shift = feats_all[t.me].astype(F32)[:, 0:1]
+    band = 16
+    bands = LIVE // band
+
+    def sums_of(count, block_at, carry):
+        out = []
+        for r in range(bands):
+            rows = pl.ds(r * band, band)
+            about = jnp.broadcast_to(shift[r * band : (r + 1) * band], (band, LANES))
+
+            def add_up(k, pair):
+                moved = feats_all[block_at(k), rows].astype(F32) - about
+                return pair[0] + moved, pair[1] + moved * moved
+
+            out.append(lax.fori_loop(0, count, add_up, carry[r], unroll=8))
+        return out
+
+    def line(off):
+        return lambda k: t.block(k, t.turn(t.q, off))
+
+    zero = jnp.zeros((band, LANES), F32)
+    sums = [(zero, zero)] * bands
+    g_feats.hop0()
+    sums = sums_of(n, line(0), sums)
     embed(1)
     text_packed = dot(text_own[...], perm)
     text_a = text_packed[:, 0:LANES]
     text_b_tile = text_packed[:, LANES : 2 * LANES]
     ta_all[t.me] = text_a.astype(BF16)
     g_ta.start()
-
-    g_feats.hop0()
-    g_feats.hop(1)
-    g_feats.hop(2)
-    g_feats.hop(3)
+    g_feats.relay()
     g_og.hop0()
-    g_feats.hop(4)
-
-    shift = feats_all[t.me].astype(F32)[:, 0:1]
-
-    band = 16
-    bands = LIVE // band
-
-    def sums_of(core, carry):
-        out = []
-        for r in range(bands):
-            rows = pl.ds(r * band, band)
-            about = jnp.broadcast_to(shift[r * band : (r + 1) * band], (band, LANES))
-
-            def add_up(k, pair):
-                moved = feats_all[2 * k + core, rows].astype(F32) - about
-                return pair[0] + moved, pair[1] + moved * moved
-
-            out.append(lax.fori_loop(0, blocks // 2, add_up, carry[r], unroll=8))
-        return out
-
-    zero = jnp.zeros((band, LANES), F32)
-    sums = sums_of(t.c, [(zero, zero)] * bands)
+    for off in (2, -2):
+        sums = sums_of(n, line(off), sums)
+    g_feats.tail(1)
+    for off in (1, -1):
+        sums = sums_of(n, line(off), sums)
+    g_feats.tail(3)
+    for off in (3, -3):
+        sums = sums_of(n, line(off), sums)
+    g_feats.tail4()
+    sums = sums_of(n, line(n // 2), sums)
     g_feats.finish()
-    sums = sums_of(1 - t.c, sums)
+    sums = sums_of(blocks // 2, lambda k: 2 * k + 1 - t.c, sums)
     sums = [jnp.concatenate([sums[r][e] for r in range(bands)], axis=0) for e in range(2)]
     inside = lax.broadcasted_iota(jnp.int32, (LIVE, LANES), 1) < width
     off = jnp.sum(jnp.where(inside, sums[0], 0.0), axis=1, keepdims=True) / pix
@@ -651,7 +693,7 @@
         return acc + dot(wpad[:, span], jnp.concatenate(tiles, axis=1), NT)
 
     hidden = lax.fori_loop(
-        0, blocks // fold, first_step, jnp.zeros((cols, LIVE), F32), unroll=2
+        0, blocks // fold, first_step, jnp.zeros((cols, LIVE), F32), unroll=4
     )
     hidden = 0.5 * hidden * (1.0 + erf(hidden * 0.7071067811865476))
     act_all[t.me] = jnp.zeros((cols, LANES), BF16)
@@ -660,6 +702,7 @@
 
     loads[1].wait()
     loads[2].wait()
+    smalls[6].wait()
     big_eye = jnp.where(
         lax.broadcasted_iota(jnp.int32, (seq, seq), 1)
         == lax.broadcasted_iota(jnp.int32, (seq, seq), 0),
@@ -770,11 +813,14 @@
         return inv, dots, both
 
     def spread_out(both, scatter):
-        @pl.loop(0, 8, unroll=2)
-        def _(k):
-            at_row = pl.multiple_of(k * span_rows, span_rows)
-            value = dot(wcat[pl.ds(at_row, span_rows), :], both)
-            value = value.reshape(group // 2, 2, cols, LANES)
+        some = 2 * group
+        part_rows = some * cols
+
+        @pl.loop(0, blocks // some)
+        def _(k):
+            at_row = pl.multiple_of(k * part_rows, part_rows)
+            value = dot(wcat[pl.ds(at_row, part_rows), :], both)
+            value = value.reshape(some // 2, 2, cols, LANES)
             scatter.fill(k, value[:, 0], value[:, 1])
 
     g_ta.finish()
@@ -906,7 +952,6 @@
     model = blocks * cols
     half = n // 2
     vmem = pl.BlockSpec(memory_space=pltpu.VMEM)
-    smem = pl.BlockSpec(memory_space=pltpu.SMEM)
     hbm = pl.BlockSpec(memory_space=pl.ANY)
     dma = pltpu.SemaphoreType.DMA
     tile = (cols, LANES)
@@ -918,24 +963,17 @@
             jax.ShapeDtypeStruct((cols, LANES), BF16),
             jax.ShapeDtypeStruct((blocks, *tile), BF16),
         ),
-        in_specs=[
-            vmem,
-            smem,
-            vmem,
-            smem,
-            vmem,
-            vmem,
-            hbm,
-            hbm,
-            hbm,
-            vmem,
-            hbm,
-            hbm,
-            hbm,
-            vmem,
-        ],
+        in_specs=[hbm] * 14,
         out_specs=(vmem, vmem, hbm),
         scratch_shapes=[
+            pltpu.VMEM(image_features.shape[::-1], BF16),
+            pltpu.SMEM(image_counts.shape, jnp.int32),
+            pltpu.VMEM((1, slot_position.shape[0]), jnp.int32),
+            pltpu.SMEM(text_ids.shape, jnp.int32),
+            pltpu.VMEM((norm_gain.shape[0] // LANES, LANES), F32),
+            pltpu.VMEM((norm_bias.shape[0] // LANES, LANES), F32),
+            pltpu.VMEM((1, model), F32),
+            pltpu.VMEM((cols, seq), BF16),
             pltpu.VMEM(proj_first.shape, BF16),
             pltpu.VMEM(proj_second.shape, BF16),
             pltpu.VMEM((embedding.shape[1] // LANES, cols, LANES), BF16),
@@ -966,6 +1004,7 @@
             pltpu.VMEM((8, LANES), F32),
             pltpu.VMEM((n, 8, LANES), F32),
             dma((7,)),
+            dma((8,)),
             dma((5, half)),
             dma((5, n - 1, half)),
             dma((5, 1)),

time: 111 us -> 102 us (0.919)
  Pallas kernels: 110 us -> 100 us
    pallas_call x1, Pallas kernels: 107 us -> 97.6 us  [on_device(): pl.pallas_call(kernel_body, out_shape=(jax.ShapeDtypeStruct((cols, seq),...]
where the time goes in v3:
time: 102 us; the launch traced here: 101 us
  Pallas kernels  100 us (98%)
    pallas_call x1, Pallas kernels, on_device(): pl.pallas_call(kernel_body, out_shape=(jax.ShapeDtypeStruct((cols, seq),...  97.6 us
    pallas_call x1, Pallas kernels, on_device(): pl.pallas_call(second_grad_body, grid=(parts,), out_shape=(jax.ShapeDtype...  2.75 us

profile of v3, /device:TPU:514, one launch (start us, length us, event | category | flops | bytes accessed | tf_op | source)
XLA Modules:
  0.0 101.0 jit_solution(14648031823893310402)
XLA Ops:
  0.6 97.6 %projector_step.1 = (f32[48,256]{1,0:T(8,128)}, bf16[48,128]{1,0:T(8,128)(2,1)}, bf16[128,48,128]{2,1,0:T(8,128)(2,1)}) custom-call(bf16[100,128]{1,0:T(8,128)(2,1)} %bitcast.11, s32[2]{0:T(128)} %counts_hbm.1, s32[1,128]{1,0:T(1,128)} %bitcast.14, s32[256]{0:T(256)} %ids_hbm.1, f32[100,128]{1,0:T(8,128)} %bitcast.9, f32[100,128]{1,0:T(8,128)} %bitcast.10, ...), custom_call_target="tpu_custom_call" | custom-call | tf_op jit(solution)/shard_map/projector_step/pallas_call | solution.py:959
  98.3 2.7 %second_grad.1 = (f32[48,6144]{1,0:T(8,128)}, f32[48,256]{1,0:T(8,128)}) custom-call(bf16[48,128]{1,0:T(8,128)(2,1)} %get-tuple-element.7.pgrad_ref, bf16[6144,128]{1,0:T(8,128)(2,1)} %bitcast.8, f32[48,256]{1,0:T(8,128)} %get-tuple-element.9.igrad_in), custom_call_target="tpu_custom_call" | custom-call | tf_op jit(solution)/shard_map/second_grad/pallas_call | solution.py:1040
